TPU v7x, 32 devices: a whole 2x2x4 slice. The times are simulated.
32 devices in a mesh: seq: 8 (over z, y), tp: 4 (over x, core).
Axes of the slice: x: 2, y: 2, z: 4, core: 2. Of those that a mesh axis runs over, the one named last changes fastest.
Arguments:
- tokens: bfloat16 [4096, 2048], P('seq'), may hold values from -16 to 16
- forget: float32 [4096, 32], P('seq', 'tp'), may hold values from -5 to 0, as said below
- attn_gain: float32 [2048], replicated, may hold values from 0.1 to 1.9
- projections: bfloat16 [3, 2048, 2048], P(None, None, 'tp'), may hold values from -0.125 to 0.125
- out_weight: bfloat16 [2048, 2048], P('tp'), may hold values from -0.125 to 0.125
- ffn_gain: float32 [2048], replicated, may hold values from 0.1 to 1.9
- expand_weight: bfloat16 [2, 2048, 4096], P(None, None, 'tp'), may hold values from -0.125 to 0.125
- down_weight: bfloat16 [4096, 2048], P('tp'), may hold values from -0.09375 to 0.09375
Outputs:
- output: bfloat16 [4096, 2048], P('seq')
Inputs may be any that keep to these rules, and one draw needn't show every extreme that they name: forget is never positive.
All inputs are finite; a program needn't handle non-finite values.
Results may differ from a plain program's by a relative error of at most 0.011.
Values may be sent and summed in bfloat16 or wider, within the bound.
No kernel may reach another device: no remote copies, remote signals or barrier semaphores. Data moves between devices by JAX's collectives and lax.ppermute only.
A program may use at most 128 MiB of HBM per device.

v0:
```python
import math

import jax
import jax.numpy as jnp
from jax import lax
from jax.sharding import PartitionSpec as P

norm_epsilon = 1e-05
head_epsilon = 1e-06


def carried_in(value, axis, join, neutral):
    count, mine = (lax.axis_size(axis), lax.axis_index(axis))
    pieces = jax.tree.map(lambda part: lax.all_gather(part, axis), value)
    running = jax.tree.map(
        lambda part, zero: jnp.full_like(part, 0) + jnp.asarray(zero, part.dtype), value, neutral
    )

    def hop(position, running):
        longer = join(running, jax.tree.map(lambda part: part[position], pieces))
        return jax.tree.map(lambda new, old: jnp.where(position < mine, new, old), longer, running)

    return lax.fori_loop(0, count - 1, hop, running)


def rms_scale(values, gain_vector):
    widened = values.astype(jnp.float32)
    mean_square = jnp.mean(widened * widened, axis=-1, keepdims=True)
    return (widened * lax.rsqrt(mean_square + norm_epsilon) * gain_vector).astype(jnp.bfloat16)


def summarize(key_rows, value_rows, forget_rows):
    log_decay = jnp.cumsum(forget_rows, axis=0)
    block_total = log_decay[-1]
    shrink_factors = jnp.exp(block_total[None, :] - log_decay)
    scaled_keys = (key_rows.astype(jnp.float32) * shrink_factors[:, :, None]).astype(jnp.bfloat16)
    block_state = jnp.einsum(
        "shd,she->hde", scaled_keys, value_rows, preferred_element_type=jnp.float32
    )
    return (log_decay, block_total, block_state)


def local_attention(query_rows, key_rows, value_rows, log_decay):
    head_size = query_rows.shape[2]
    score_scale = 1.0 / math.sqrt(head_size)
    scores = (
        jnp.einsum("thd,shd->hts", query_rows, key_rows, preferred_element_type=jnp.float32)
        * score_scale
    )
    log_gaps = log_decay.T[:, :, None] - log_decay.T[:, None, :]
    row_order = jnp.arange(query_rows.shape[0])
    causal = (row_order[:, None] >= row_order[None, :])[None]
    local_weights = jnp.where(
        causal, scores * jnp.exp(jnp.where(causal, log_gaps, 0.0)), 0.0
    ).astype(jnp.bfloat16)
    return jnp.einsum("hts,she->the", local_weights, value_rows, preferred_element_type=jnp.float32)


def finish_heads(query_rows, local_part, log_decay, incoming):
    head_size = query_rows.shape[2]
    score_scale = 1.0 / math.sqrt(head_size)
    carried = jnp.einsum(
        "thd,hde->the", query_rows.astype(jnp.float32), incoming, precision=lax.Precision.HIGHEST
    )
    attended = local_part + carried * (jnp.exp(log_decay) * score_scale)[:, :, None]
    mean_square = jnp.mean(attended * attended, axis=-1, keepdims=True)
    head_out = (attended * lax.rsqrt(mean_square + head_epsilon)).astype(jnp.bfloat16)
    return head_out.reshape(query_rows.shape[0], -1)


def feed_forward(rows_in, expand_weight):
    gate_proj = jnp.dot(rows_in, expand_weight[0], preferred_element_type=jnp.float32)
    up_proj = jnp.dot(rows_in, expand_weight[1], preferred_element_type=jnp.float32)
    return (jax.nn.silu(gate_proj) * up_proj).astype(jnp.bfloat16)


def local(tokens, forget, attn_gain, projections, out_weight, ffn_gain, expand_weight, down_weight):
    row_count = tokens.shape[0]
    head_count = forget.shape[1]
    head_size = projections.shape[2] // head_count
    normed = rms_scale(tokens, attn_gain)
    shaped = []
    for which in range(3):
        projected = jnp.dot(normed, projections[which], preferred_element_type=jnp.float32).astype(
            jnp.bfloat16
        )
        shaped.append(projected.reshape(row_count, head_count, head_size))
    query_rows, key_rows, value_rows = shaped
    log_decay, block_total, block_state = summarize(key_rows, value_rows, forget)

    def combine(earlier, following):
        return (earlier[0] * following[0], following[0][:, None, None] * earlier[1] + following[1])

    identity = (jnp.ones_like(block_total), jnp.zeros_like(block_state))
    _, incoming = carried_in((jnp.exp(block_total), block_state), "seq", combine, identity)
    local_part = local_attention(query_rows, key_rows, value_rows, log_decay)
    head_out = finish_heads(query_rows, local_part, log_decay, incoming)
    row_share = row_count // lax.axis_size("tp")
    tp_index = lax.axis_index("tp")
    own_tokens = lax.dynamic_slice_in_dim(tokens, tp_index * row_share, row_share, 0)
    picked = head_out
    attn_summed = lax.psum_scatter(
        jnp.dot(picked, out_weight, preferred_element_type=jnp.float32),
        "tp",
        scatter_dimension=0,
        tiled=True,
    )
    residual = (own_tokens.astype(jnp.float32) + attn_summed).astype(jnp.bfloat16)
    normed_ffn = rms_scale(residual, ffn_gain)
    hidden = feed_forward(lax.all_gather(normed_ffn, "tp", axis=0, tiled=True), expand_weight)
    picked = hidden
    ffn_summed = lax.psum_scatter(
        jnp.dot(picked, down_weight, preferred_element_type=jnp.float32).astype(jnp.bfloat16),
        "tp",
        scatter_dimension=0,
        tiled=True,
    ).astype(jnp.float32)
    own_output = (residual.astype(jnp.float32) + ffn_summed).astype(jnp.bfloat16)
    return lax.all_gather(own_output, "tp", axis=0, tiled=True)


def solution(mesh):
    placed = (
        P("seq", None),
        P("seq", "tp"),
        P(),
        P(None, None, "tp"),
        P("tp", None),
        P(),
        P(None, None, "tp"),
        P("tp", None),
    )
    return jax.shard_map(
        local, mesh=mesh, in_specs=placed, out_specs=P("seq", None), check_vma=False
    )
```

profile of v0, /device:TPU:0, one launch (start us, length us, event | category | flops | bytes accessed | tf_op | source)
XLA Modules:
  0.0 235.0 jit_solution(2786294146817347962)
XLA Ops:
  6.5 2.2 fusion.1
  8.8 3.8 %fusion.34 = bf16[512,512]{0,1:T(8,128)(2,1)S(1)} fusion(bf16[3,2048,512]{2,1,0:T(8,128)(2,1)} %param.13, bf16[512,2048]{1,0:T(8,128)(2,1)} %param.10, f32[2048]{0:T(1024)} %param.12, f32[512]{0:T(512)S(1)} %add_rsqrt_fusion.1), kind=kOutput, calls=%fused_computation.38 | convolution fusion | flops 1078198272 | bytes 4728832 | tf_op jit(solution)/shard_map/dot_general | solution.py:84
  12.6 3.2 %fusion.28 = bf16[512,512]{0,1:T(8,128)(2,1)S(1)} fusion(bf16[3,2048,512]{2,1,0:T(8,128)(2,1)} %param.13, bf16[512,2048]{1,0:T(8,128)(2,1)S(1)} %copy-done.1, f32[2048]{0:T(1024)S(1)} %copy-done.6, f32[512]{0:T(512)S(1)} %add_rsqrt_fusion.1), kind=kOutput, calls=%fused_computation.36 | convolution fusion | flops 1078198272 | bytes 4728832 | tf_op jit(solution)/shard_map/dot_general | solution.py:84
  15.9 1.1 reduce-window.6
  18.7 22.3 %all-gather.1 = f32[8,1,8]{2,1,0:T(1,128)S(1)} all-gather(f32[1,1,8]{2,1,0:T(1,128)S(1)} %bitcast.80), channel_id=1, replica_groups=mesh['seq'=8,'tp'=4] {'seq'}, dimensions={0}, use_global_device_ids=true | all-gather | bytes 288 | tf_op jit(solution)/shard_map/all_gather | solution.py:14
  41.8 4.4 %fusion.31 = bf16[512,512]{0,1:T(8,128)(2,1)} fusion(bf16[3,2048,512]{2,1,0:T(8,128)(2,1)} %param.13, bf16[512,2048]{1,0:T(8,128)(2,1)} %param.10, f32[2048]{0:T(1024)S(1)} %copy-done.6, f32[512]{0:T(512)S(1)} %add_rsqrt_fusion.1), kind=kOutput, calls=%fused_computation.37 | convolution fusion | flops 1078198272 | bytes 4728832 | tf_op jit(solution)/shard_map/dot_general | solution.py:84
  46.2 5.4 %fusion.25 = f32[512,8,64]{0,2,1:T(8,128)S(1)} fusion(bf16[512,8,64]{0,2,1:T(8,128)(2,1)} %bitcast.77, f32[8,512]{1,0:T(8,128)S(1)} %add_bitcast_fusion.1, pred[512,512]{1,0:T(8,128)(4,1)} %iota_compare_fusion, bf16[512,8,64]{0,2,1:T(8,128)(2,1)} %bitcast.72, bf16[512,8,64]{0,2,1:T(8,128)(2,1)} %bitcast.75), kind=kOutput, calls=%fused_computation.32 | convolution fusion | flops 549453824 | bytes 2899968 | tf_op jit(solution)/shard_map/hts,she->the/dot_general | solution.py:56
  51.6 19.1 %all-gather.10.cloned.1.call-done = f32[64,64,64]{2,1,0:T(8,128)} async-done(((f32[8,64,64]{2,1,0:T(8,128)}), f32[64,64,64]{2,1,0:T(8,128)}) %all-gather.10.cloned.1.call-update) | async-done | bytes 1048592 | tf_op jit(solution)/shard_map/all_gather | solution.py:14
  70.8 7.6 %while.14 = (s32[]{:T(128)}, f32[8,64,64]{2,1,0:T(8,128)S(1)}, s32[]{:T(128)}, f32[8,8]{1,0:T(8,128)S(1)}, f32[8,8,64,64]{3,2,1,0:T(8,128)}, /*index=5*/s32[]{:T(128)}, s32[]{:T(128)}) while((s32[]{:T(128)}, f32[8,64,64]{2,1,0:T(8,128)S(1)}, s32[]{:T(128)}, f32[8,8]{1,0:T(8,128)S(1)}, f32[8,8,64,64]{3,2,1,0:T(8,128)}, ...), condition=%wide.region_4.5_spmd.clone, body=%wide.region_3.4_spmd.clone.sunk | while | flops 131076 | bytes 393425 | solution.py:23
  71.9 1.1 fusion.65
  73.0 1.1 fusion.65
  74.0 1.1 fusion.65
  75.1 1.1 fusion.65
  78.4 1.8 multiply_reduce_fusion
  80.4 3.2 %fusion.52 = f32[512,2048]{1,0:T(8,128)} fusion(bf16[512,512]{0,1:T(8,128)(2,1)S(1)} %bitcast.70, bf16[512,2048]{1,0:T(8,128)(2,1)S(1)} %copy-done), kind=kOutput, calls=%fused_computation.64 | convolution fusion | flops 1073741824 | bytes 6815744 | tf_op jit(solution)/shard_map/dot_general | solution.py:103
  83.7 43.2 %reduce-scatter.3.cloned.1.call-done = f32[128,2048]{1,0:T(8,128)} async-done(((f32[512,2048]{1,0:T(8,128)}), f32[128,2048]{1,0:T(8,128)}) %reduce-scatter.3.cloned.1.call-update) | async-done | bytes 1048592 | tf_op jit(solution)/shard_map/reduce_scatter | solution.py:102
  126.8 1.6 fusion.39
  129.7 22.5 %all-gather.6.cloned.1.call-done = bf16[512,2048]{1,0:T(8,128)(2,1)} async-done(((bf16[128,2048]{1,0:T(8,128)(2,1)}), bf16[512,2048]{1,0:T(8,128)(2,1)}) %all-gather.6.cloned.1.call-update) | async-done | bytes 2097168 | tf_op jit(solution)/shard_map/all_gather | solution.py:110
  152.2 6.5 %fusion.6 = f32[512,1024]{1,0:T(8,128)} fusion(bf16[512,2048]{1,0:T(8,128)(2,1)} %all-gather.6.cloned.1.call-done, bf16[2,2048,1024]{2,1,0:T(8,128)(2,1)} %param.16), kind=kOutput, calls=%fused_computation.11 | convolution fusion | flops 2147483648 | bytes 8388608 | tf_op jit(solution)/shard_map/dot_general | solution.py:72
  158.7 10.6 %convolution_convert_fusion = bf16[512,2048]{1,0:T(8,128)(2,1)} fusion(bf16[1024,2048]{1,0:T(8,128)(2,1)} %param.17, f32[512,1024]{1,0:T(8,128)} %fusion.6, bf16[512,2048]{1,0:T(8,128)(2,1)} %all-gather.6.cloned.1.call-done, bf16[2,2048,1024]{2,1,0:T(8,128)(2,1)} %param.16), kind=kOutput, calls=%fused_computation.18 | convolution fusion | flops 4299161600 | bytes 14680064 | tf_op jit(solution)/shard_map/dot_general | solution.py:113
  169.3 31.3 %reduce-scatter.5.cloned.1.call-done = bf16[128,2048]{1,0:T(8,128)(2,1)} async-done(((bf16[512,2048]{1,0:T(8,128)(2,1)}), bf16[128,2048]{1,0:T(8,128)(2,1)}) %reduce-scatter.5.cloned.1.call-update) | async-done | bytes 524304 | tf_op jit(solution)/shard_map/reduce_scatter | solution.py:112
  200.6 2.0 fusion.42
  202.6 22.7 %all-gather.8.cloned.1.call-done = bf16[512,2048]{1,0:T(8,128)(2,1)} async-done(((bf16[128,2048]{1,0:T(8,128)(2,1)}), bf16[512,2048]{1,0:T(8,128)(2,1)}) %all-gather.8.cloned.1.call-update) | async-done | bytes 2097168 | tf_op jit(solution)/shard_map/all_gather | solution.py:119
  225.3 3.2 %copy.25 = bf16[512,2048]{1,0:T(8,128)(2,1)} copy(bf16[512,2048]{1,0:T(8,128)(2,1)} %all-gather.8.cloned.1.call-done) | data formatting | bytes 4194304
  (49 shorter events, 7.2 us)
Async XLA Ops:
  6.5 73.8 %copy-start = (bf16[512,2048]{1,0:T(8,128)(2,1)S(1)}, bf16[512,2048]{1,0:T(8,128)(2,1)}, u32[]{:S(2)}) copy-start(bf16[512,2048]{1,0:T(8,128)(2,1)} %param.14) | copy-start | bytes 6291460
  6.5 64.2 %all-gather.10.cloned.1.call-start = ((), (), s32[]{:S(2)}) async-start(), calls=%async_computation.6 | async-start | bytes 2359296 | tf_op jit(solution)/shard_map/all_gather | solution.py:14
  8.8 3.8 %copy-start.1 = (bf16[512,2048]{1,0:T(8,128)(2,1)S(1)}, bf16[512,2048]{1,0:T(8,128)(2,1)}, u32[]{:S(2)}) copy-start(bf16[512,2048]{1,0:T(8,128)(2,1)} %param.10) | copy-start | bytes 6291460
  8.8 3.8 %copy-start.6 = (f32[2048]{0:T(1024)S(1)}, f32[2048]{0:T(1024)}, u32[]{:S(2)}) copy-start(f32[2048]{0:T(1024)} %param.12) | copy-start | bytes 24580
  12.6 5.0 %copy-start.2 = (bf16[512,512]{0,1:T(8,128)(2,1)}, bf16[512,512]{0,1:T(8,128)(2,1)S(1)}, u32[]{:S(2)}) copy-start(bf16[512,512]{0,1:T(8,128)(2,1)S(1)} %fusion.34) | copy-start | bytes 1572868
  12.6 3.3 %copy-start.4 = (f32[512,8]{0,1:T(8,128)S(1)}, f32[512,8]{0,1:T(8,128)}, u32[]{:S(2)}) copy-start(f32[512,8]{0,1:T(8,128)} %param.11) | copy-start | bytes 49156
  15.8 30.4 %copy-start.3 = (bf16[512,512]{0,1:T(8,128)(2,1)}, bf16[512,512]{0,1:T(8,128)(2,1)S(1)}, u32[]{:S(2)}) copy-start(bf16[512,512]{0,1:T(8,128)(2,1)S(1)} %fusion.28) | copy-start | bytes 1572868
  18.6 108.2 %reduce-scatter.3.cloned.1.call-start = ((), (), s32[]{:S(2)}) async-start(), calls=%async_computation.2 | async-start | bytes 5242880 | tf_op jit(solution)/shard_map/reduce_scatter | solution.py:102
  83.6 44.9 %copy-start.5 = (f32[2048]{0:T(1024)S(1)}, f32[2048]{0:T(1024)}, u32[]{:S(2)}) copy-start(f32[2048]{0:T(1024)} %param.15) | copy-start | bytes 24580
  83.6 68.6 %all-gather.6.cloned.1.call-start = ((), (), s32[]{:S(2)}) async-start(), calls=%async_computation.3 | async-start | bytes 2621440 | tf_op jit(solution)/shard_map/all_gather | solution.py:110
  129.5 71.2 %reduce-scatter.5.cloned.1.call-start = ((), (), s32[]{:S(2)}) async-start(), calls=%async_computation.4 | async-start | bytes 2621440 | tf_op jit(solution)/shard_map/reduce_scatter | solution.py:112
  169.3 56.0 %all-gather.8.cloned.1.call-start = ((), (), s32[]{:S(2)}) async-start(), calls=%async_computation.5 | async-start | bytes 2621440 | tf_op jit(solution)/shard_map/all_gather | solution.py:119
Sparse Core Ops, SparseCore 0:
  18.7 51.9 all-gather.9
  83.7 43.0 reduce-scatter.2
  129.6 22.5 all-gather.5
  169.4 31.1 reduce-scatter.4
  202.7 22.5 all-gather.7
where the time goes:
time: 236 us; the launch traced here: 235 us
  waiting for transfers between devices  139 us (59%)
  matrix products  39.8 us (17%)
  blocking collectives  22.3 us (9%)
  other arithmetic  16.5 us (7%)
  between operations  13.3 us (6%)
  local copies, waits for them, and re-layouts  3.6 us (2%)
    reduce_scatter x1, waiting for transfers between devices, local(): lax.psum_scatter(jnp.dot(picked, out_weight, preferred_element_type=jnp.f...  43.2 us
    reduce_scatter x1, waiting for transfers between devices, local(): lax.psum_scatter(jnp.dot(picked, down_weight, preferred_element_type=jnp....  31.3 us
    all_gather x1, waiting for transfers between devices, local(): return lax.all_gather(own_output, 'tp', axis=0, tiled=True)  22.7 us
    all_gather x1, waiting for transfers between devices, local(): lax.all_gather(normed_ffn, 'tp', axis=0, tiled=True)  22.5 us
    all_gather x1, blocking collectives, carried_in(): pieces = jax.tree.map(lambda part: lax.all_gather(part, axis), value)  22.3 us
    all_gather x1, waiting for transfers between devices, carried_in(): pieces = jax.tree.map(lambda part: lax.all_gather(part, axis), value)  19.1 us
    dot_general x3, matrix products, local(): jnp.dot(normed, projections[which], preferred_element_type=jnp.float32)  11.4 us
    dot_general x1, matrix products, local(): jnp.dot(picked, down_weight, preferred_element_type=jnp.float32)  10.6 us
  transfers between devices with their start and end apart: 5, of which 5 were waited for; matrix products, arithmetic and copies ran while one was open for 5% of the time, Pallas kernels for 0%

commit v1 on v0

v1 whole, which is shorter than its diff:
```python
import functools
import math

import jax
import jax.numpy as jnp
from jax import lax
from jax.experimental import pallas as pl
from jax.experimental.pallas import tpu as pltpu
from jax.sharding import PartitionSpec as P

norm_epsilon = 1e-05
head_epsilon = 1e-06
cores = 2
log2e = 1.4426950408889634

f32, bf16 = jnp.float32, jnp.bfloat16


vmem = pl.BlockSpec(memory_space=pltpu.VMEM)
smem = pl.BlockSpec(memory_space=pltpu.SMEM)
hbm = pl.BlockSpec(memory_space=pltpu.HBM)


def cost(flops):
    return pl.CostEstimate(flops=flops, bytes_accessed=0, transcendentals=0)


def room(mebibytes):
    return pltpu.CompilerParams(vmem_limit_bytes=mebibytes << 20)


def scalar(value):
    return value.astype(jnp.int32).reshape(1)


def iota(shape, axis):
    return lax.broadcasted_iota(jnp.int32, shape, axis)


def dot(a, b):
    return jnp.dot(a, b, preferred_element_type=f32)


def contract(a, b, dim_a, dim_b):
    return lax.dot_general(a, b, (((dim_a,), (dim_b,)), ((), ())), preferred_element_type=f32)


def split3(value):
    high = value.astype(bf16)
    rest = value - high.astype(f32)
    middle = rest.astype(bf16)
    return high, middle, (rest - middle.astype(f32)).astype(bf16)


def normalize(rows, gain):
    mean_square = jnp.mean(rows * rows, axis=-1, keepdims=True)
    return (rows * lax.rsqrt(mean_square + norm_epsilon) * gain).astype(bf16)


def spread_heads(sums, size):
    heads = sums.shape[1]
    spread = (iota((heads, heads * size), 1) // size == iota((heads, heads * size), 0)).astype(bf16)
    parts = split3(sums)
    return dot(parts[0], spread) + dot(parts[1], spread) + dot(parts[2], spread)


def swap_cores(value):
    count = lax.axis_size("tp")
    return lax.ppermute(value, "tp", [(i, i ^ 1) for i in range(count)])


def across_chips(value):
    count = lax.axis_size("tp")
    return lax.ppermute(value, "tp", [(i, (i + cores) % count) for i in range(count)])


def with_seq(value, bit):
    count = lax.axis_size("seq")
    return lax.ppermute(value, "seq", [(i, i ^ bit) for i in range(count)])


def cut_kernel(group, source, *refs):
    outs, sems = refs[:-1], refs[-1]
    share = outs[0].shape[1]
    loads = []
    for at, out in enumerate(outs):
        columns = pl.ds(pl.multiple_of((len(outs) * group[0] + at) * share, share), share)
        loads.append(pltpu.make_async_copy(source.at[:, columns], out, sems.at[at]))
    for load in loads:
        load.start()
    for load in loads:
        load.wait()


def cut_columns(group, weight, pieces):
    share = weight.shape[1] // (2 * pieces)
    return pl.pallas_call(
        cut_kernel,
        in_specs=[smem, hbm],
        out_specs=[hbm] * pieces,
        out_shape=[jax.ShapeDtypeStruct((weight.shape[0], share), weight.dtype)] * pieces,
        scratch_shapes=[pltpu.SemaphoreType.DMA((pieces,))],
        compiler_params=room(1),
        cost_estimate=cost(1 << 30),
        name="cut_columns",
    )(scalar(group), weight)


def project_kernel(
    size, tok, gain, forget, weight, keys, values, normed, query_weight, column, row, state, sent, tok_here, weight_here, sems
):
    heads, rows = forget.shape
    parts = 4
    span = rows // parts
    loads = [
        pltpu.make_async_copy(tok.at[pl.ds(p * span, span)], tok_here.at[pl.ds(p * span, span)], sems.at[p])
        for p in range(parts)
    ]
    for which in (1, 2):
        loads.append(pltpu.make_async_copy(weight.at[which], weight_here.at[which - 1], sems.at[parts + which - 1]))
    loads.append(pltpu.make_async_copy(weight.at[0], query_weight, sems.at[parts + 2]))
    for load in loads:
        load.start()

    pieces = split3(forget[...])
    upper = (iota((rows, rows), 0) <= iota((rows, rows), 1)).astype(bf16)
    sums = (dot(pieces[0], upper) + dot(pieces[1], upper) + dot(pieces[2], upper)) * log2e
    row[...] = sums
    by_token = jnp.transpose(sums)
    column[...] = by_token
    grown = spread_heads(by_token, size)
    ends = grown[rows - 1 :, :]
    decays = jnp.exp2(ends)

    for p in range(parts):
        loads[p].wait()
        here = pl.ds(p * span, span)
        normed[here, :] = normalize(tok_here[here, :].astype(f32), gain[...])
    loads[parts].wait()
    keys[...] = dot(normed[...], weight_here[0]).astype(bf16)
    loads[parts + 1].wait()
    values[...] = dot(normed[...], weight_here[1]).astype(bf16)

    lanes = 2 * size
    first = iota((size, lanes), 1) < size
    picked = jnp.zeros((16, lanes), f32)
    for pair in range(heads // 2):
        cut = slice(pair * lanes, (pair + 1) * lanes)
        shrink = jnp.exp2(ends[:, cut] - grown[:, cut])
        scaled = (keys[:, cut].astype(f32) * shrink).astype(bf16)
        both = contract(scaled, values[:, cut], 0, 0)
        compact = jnp.where(first, both[:size], both[size:])
        state[pl.ds(pair * size, size), :] = compact
        sent[pl.ds(pair * size, size), :] = compact.astype(bf16)
        picked = jnp.where(iota((16, lanes), 0) == pair, jnp.broadcast_to(decays[:, cut], (16, lanes)), picked)
    base = heads // 2 * size
    state[pl.ds(base, 16), :] = picked
    sent[pl.ds(base, 16), :] = picked.astype(bf16)
    loads[parts + 2].wait()


def project(tokens, gain, forget, projections, size):
    rows, width = tokens.shape
    heads = forget.shape[1]
    mine = projections.shape[2]
    packed = (heads // 2 * size + 16, 2 * size)
    outs = [
        ((rows, mine), bf16),
        ((rows, mine), bf16),
        ((rows, width), bf16),
        ((width, mine), bf16),
        ((rows, heads), f32),
        ((heads, rows), f32),
        (packed, f32),
        (packed, bf16),
    ]
    return pl.pallas_call(
        functools.partial(project_kernel, size),
        in_specs=[hbm, vmem, vmem, hbm],
        out_specs=[vmem] * len(outs),
        out_shape=[jax.ShapeDtypeStruct(shape, kind) for shape, kind in outs],
        scratch_shapes=[
            pltpu.VMEM((rows, width), bf16),
            pltpu.VMEM((2, width, mine), bf16),
            pltpu.SemaphoreType.DMA((7,)),
        ],
        cost_estimate=cost(4 * rows * width * mine),
        compiler_params=room(24),
        name="project",
    )(tokens, gain.reshape(1, width), forget.T, projections)


def query_kernel(scale, normed, weight, out):
    out[...] = (dot(normed[...], weight[...]).astype(bf16).astype(f32) * scale).astype(bf16)


def queries(normed, weight, size):
    rows, width = normed.shape
    mine = weight.shape[1]
    return pl.pallas_call(
        functools.partial(query_kernel, 1.0 / math.sqrt(size)),
        in_specs=[vmem] * 2,
        out_specs=vmem,
        out_shape=jax.ShapeDtypeStruct((rows, mine), bf16),
        cost_estimate=cost(2 * rows * width * mine),
        compiler_params=room(8),
        name="queries",
    )(normed, weight)


def block_kernel(size, first_pair, pairs, q, k, v, column, row, out):
    rows, lanes = q.shape[0], 2 * size
    span = rows // 2
    below = iota((span, span), 0) >= iota((span, span), 1)
    for at in range(pairs):
        cut = slice((first_pair + at) * lanes, (first_pair + at + 1) * lanes)
        total = [None, None]
        for side in range(2):
            head = 2 * (first_pair + at) + side
            half = (iota((span, lanes), 1) // size) == side
            zero = jnp.zeros((span, lanes), bf16)
            ks = [jnp.where(half, k[pl.ds(b * span, span), cut], zero) for b in range(2)]
            vs = [jnp.where(half, v[pl.ds(b * span, span), cut], zero) for b in range(2)]
            for tb in range(2):
                here = column[pl.ds(tb * span, span), head : head + 1]
                for sb in range(tb + 1):
                    scores = contract(q[pl.ds(tb * span, span), cut], ks[sb], 1, 1)
                    gap = here - row[head : head + 1, pl.ds(sb * span, span)]
                    if sb == tb:
                        gap = jnp.where(below, gap, -jnp.inf)
                    weights = (scores * jnp.exp2(gap)).astype(bf16)
                    part = dot(weights, vs[sb])
                    total[tb] = part if total[tb] is None else total[tb] + part
        for tb in range(2):
            out[pl.ds(tb * span, span), pl.ds(at * lanes, lanes)] = total[tb]


def block_attention(q, k, v, column, row, size, part, parts):
    rows, mine = q.shape
    heads = column.shape[1]
    wide = mine // parts
    first_pair = part * (heads // 2 // parts)
    return pl.pallas_call(
        functools.partial(block_kernel, size, first_pair, heads // 2 // parts),
        in_specs=[vmem] * 5,
        out_specs=vmem,
        out_shape=jax.ShapeDtypeStruct((rows, wide), f32),
        cost_estimate=cost(16 * rows * rows * wide),
        compiler_params=room(10),
    )(q, k, v, column, row)


def combine_kernel(first, size, later, state, before, got, new_state, new_before, sent):
    tail = 16
    body, lanes = state.shape[0] - tail, state.shape[1]
    is_later = later[0] != 0
    rest = pl.ds(body, tail)
    mine_decay, got_decay = state[rest, :], got[rest, :].astype(f32)
    early_decay = jnp.ones((tail, lanes), f32) if first else before[rest, :]
    for pair in range(body // size):
        at = pl.ds(pair * size, size)
        theirs, own = got[at, :].astype(f32), state[at, :]
        prior = jnp.zeros((size, lanes), f32) if first else before[at, :]
        d_mine, d_got, d_early = (x[pair : pair + 1] for x in (mine_decay, got_decay, early_decay))
        fresh = jnp.where(is_later, d_mine * theirs + own, d_got * own + theirs)
        new_state[at, :] = fresh
        sent[at, :] = fresh.astype(bf16)
        new_before[at, :] = jnp.where(is_later, prior + d_early * theirs, prior)
    decay = mine_decay * got_decay
    new_state[rest, :] = decay
    sent[rest, :] = decay.astype(bf16)
    new_before[rest, :] = jnp.where(is_later, early_decay * got_decay, early_decay)


def combine(first, size, later, state, before, got):
    shape = state.shape
    return pl.pallas_call(
        functools.partial(combine_kernel, first, size),
        in_specs=[smem] + [vmem] * 3,
        out_specs=[vmem] * 3,
        out_shape=[
            jax.ShapeDtypeStruct(shape, f32),
            jax.ShapeDtypeStruct(shape, f32),
            jax.ShapeDtypeStruct(shape, bf16),
        ],
        compiler_params=room(2),
        cost_estimate=cost(1 << 28),
        name="combine",
    )(scalar(later), state, before, got)


def incoming_state(state, sent, size):
    count, mine = lax.axis_size("seq"), lax.axis_index("seq")
    before, bit = state, 1
    while bit < count:
        got = with_seq(sent, bit)
        state, before, sent = combine(bit == 1, size, mine & bit, state, before, got)
        bit *= 2
    return before


def heads_kernel(size, parts, half, q, column, before, *refs):
    locals_, out = refs[:parts], refs[parts]
    span, lanes = out.shape[0], 2 * size
    width = q.shape[1] // parts
    here = pl.ds(pl.multiple_of(half[0] * span, span), span)
    ones = (iota((lanes, lanes), 0) // size == iota((lanes, lanes), 1) // size).astype(bf16)
    first = iota((size, lanes), 1) < size
    growth = jnp.exp2(spread_heads(column[here, :], size))
    for pair in range(q.shape[1] // lanes):
        cut = slice(pair * lanes, (pair + 1) * lanes)
        compact = before[pl.ds(pair * size, size), :]
        upper = jnp.where(first, compact, 0.0).astype(bf16)
        under = jnp.where(first, 0.0, compact).astype(bf16)
        block = jnp.concatenate([upper, under], axis=0)
        carried = dot(q[here, cut], block) * growth[:, cut]
        at = pair * lanes % width
        attended = locals_[pair * lanes // width][here, at : at + lanes] + carried
        square = attended * attended
        high = square.astype(bf16)
        low = (square - high.astype(f32)).astype(bf16)
        mean_square = (dot(high, ones) + dot(low, ones)) * (1.0 / size)
        out[:, cut] = (attended * lax.rsqrt(mean_square + head_epsilon)).astype(bf16)


def finish_heads(half, q, column, before, local_parts, size):
    rows, mine = q.shape
    span = rows // cores
    return pl.pallas_call(
        functools.partial(heads_kernel, size, len(local_parts)),
        in_specs=[smem] + [vmem] * (3 + len(local_parts)),
        out_specs=vmem,
        out_shape=jax.ShapeDtypeStruct((span, mine), bf16),
        cost_estimate=cost(span * mine * 2048),
        compiler_params=room(6),
        name="finish_heads",
    )(scalar(half), q, column, before, *local_parts)


def own_heads_kernel(kept, moved, own, partner, expand_own, expand_other, out, own_here, other_here, first, second, sems):
    pairs = ((own, first), (partner, second), (expand_own, own_here), (expand_other, other_here))
    loads = [pltpu.make_async_copy(a, b, sems.at[at]) for at, (a, b) in enumerate(pairs)]
    for load in loads:
        load.start()
    for load in loads[:2]:
        load.wait()
    out[...] = dot(kept[...], first[...]) + dot(moved[...], second[...])
    for load in loads[2:]:
        load.wait()


def project_own_heads(kept, moved, own, partner, expand_own, expand_other):
    rows, depth = kept.shape
    width = own.shape[1]
    staged = jax.ShapeDtypeStruct(expand_own.shape, bf16)
    return pl.pallas_call(
        own_heads_kernel,
        in_specs=[vmem] * 2 + [hbm] * 4,
        out_specs=[vmem] * 3,
        out_shape=[jax.ShapeDtypeStruct((rows, width), f32), staged, staged],
        scratch_shapes=[pltpu.VMEM(own.shape, bf16), pltpu.VMEM(own.shape, bf16), pltpu.SemaphoreType.DMA((4,))],
        cost_estimate=cost(4 * rows * depth * width),
        compiler_params=room(8),
        name="project_own_heads",
    )(kept, moved, own, partner, expand_own, expand_other)


def far_heads_kernel(parity, kept, moved, *refs):
    weights, (sums, out) = refs[:8], refs[8:]
    share = weights[0].shape[1]
    for at in range(4):
        group = parity[0] if at < 2 else 1 - parity[0]
        here = pl.ds(pl.multiple_of((2 * group + at % 2) * share, share), share)
        part = dot(kept[...], weights[2 * at][...]) + dot(moved[...], weights[2 * at + 1][...])
        out[:, here] = sums[:, here] + part


def project_far_heads(parity, kept, moved, weights, sums):
    rows, depth = kept.shape
    width = sums.shape[1]
    return pl.pallas_call(
        far_heads_kernel,
        in_specs=[smem] + [vmem] * 11,
        out_specs=vmem,
        out_shape=jax.ShapeDtypeStruct(sums.shape, f32),
        input_output_aliases={11: 0},
        cost_estimate=cost(4 * rows * depth * width),
        compiler_params=room(12),
        name="project_far_heads",
    )(scalar(parity), kept, moved, *weights, sums)


def residual_kernel(core, tok, sums, gain, residual, normed):
    rows = sums.shape[0]
    here = pl.ds(pl.multiple_of(core[0] * rows, rows), rows)
    total = (tok[here, :].astype(f32) + sums[...]).astype(bf16)
    residual[...] = total
    normed[...] = normalize(total.astype(f32), gain[...])


def add_residual(core, tokens, sums, gain):
    shape = jax.ShapeDtypeStruct(sums.shape, bf16)
    return pl.pallas_call(
        residual_kernel,
        in_specs=[smem] + [vmem] * 3,
        out_specs=[vmem] * 2,
        out_shape=[shape, shape],
        cost_estimate=cost(sums.size * 1024),
        compiler_params=room(10),
        name="add_residual",
    )(scalar(core), tokens, sums, gain.reshape(1, -1))


def expand_kernel(rows_in, own, other, down_own, down_other, out, own_here, other_here, sems):
    pairs = ((down_own, own_here), (down_other, other_here))
    loads = [pltpu.make_async_copy(a, b, sems.at[at]) for at, (a, b) in enumerate(pairs)]
    for load in loads:
        load.start()
    hidden = own.shape[2]
    wide = hidden // 2
    for place, weight in enumerate((own, other)):
        for at in range(0, hidden, wide):
            gate = dot(rows_in[...], weight[0, :, at : at + wide])
            up = dot(rows_in[...], weight[1, :, at : at + wide])
            half_gate = 0.5 * gate
            silu = half_gate * jnp.tanh(half_gate) + half_gate
            out[:, pl.ds(place * hidden + at, wide)] = (silu * up).astype(bf16)
    for load in loads:
        load.wait()


def expand(rows_in, own, other, down_own, down_other):
    rows, width = rows_in.shape
    hidden = own.shape[2]
    staged = jax.ShapeDtypeStruct(down_own.shape, bf16)
    return pl.pallas_call(
        expand_kernel,
        in_specs=[vmem] * 3 + [hbm] * 2,
        out_specs=[vmem] * 3,
        out_shape=[jax.ShapeDtypeStruct((rows, 2 * hidden), bf16), staged, staged],
        scratch_shapes=[pltpu.SemaphoreType.DMA((2,))],
        cost_estimate=cost(8 * rows * width * hidden),
        compiler_params=room(8),
        name="expand",
    )(rows_in, own, other, down_own, down_other)


def down_kernel(start, hidden, own, other, out):
    depth, span = own.shape[0], out.shape[1]
    cut = slice(start, start + span)
    out[...] = (dot(hidden[:, :depth], own[:, cut]) + dot(hidden[:, depth:], other[:, cut])).astype(bf16)


def down(hidden, own, other, start, span):
    rows, depth = hidden.shape
    return pl.pallas_call(
        functools.partial(down_kernel, start),
        in_specs=[vmem] * 3,
        out_specs=vmem,
        out_shape=jax.ShapeDtypeStruct((rows, span), bf16),
        cost_estimate=cost(2 * rows * depth * span),
        compiler_params=room(14),
    )(hidden, own, other)


def add_kernel(start, residual, own, *refs):
    out = refs[-1]
    total = own[...].astype(f32)
    for other in refs[:-1]:
        total = total + other[...].astype(f32)
    out[...] = (residual[:, start : start + out.shape[1]].astype(f32) + total).astype(bf16)


def add_partials(start, residual, own, others):
    return pl.pallas_call(
        functools.partial(add_kernel, start),
        in_specs=[vmem] * (2 + len(others)),
        out_specs=vmem,
        out_shape=jax.ShapeDtypeStruct(own.shape, bf16),
        compiler_params=room(4),
        cost_estimate=cost(1 << 28),
        name="add_partials",
    )(residual, own, *others)


def place_kernel(count, core, *refs):
    pieces, out, sems = refs[: 2 * count], refs[-2], refs[-1]
    rows = pieces[0].shape[0]
    loads, start = [], 0
    for at in range(count):
        span = pieces[2 * at].shape[1]
        for side in range(2):
            here = pl.ds(pl.multiple_of((core[0] if side == 0 else 1 - core[0]) * rows, rows), rows)
            to = out.at[here, pl.ds(start, span)]
            loads.append(pltpu.make_async_copy(pieces[2 * at + side], to, sems.at[2 * at + side]))
        start += span
    for load in loads:
        load.start()
    for load in loads:
        load.wait()


def place(core, mine, theirs, rows):
    pieces = [x for pair in zip(mine, theirs) for x in pair]
    width = sum(x.shape[1] for x in mine)
    return pl.pallas_call(
        functools.partial(place_kernel, len(mine)),
        in_specs=[smem] + [vmem] * len(pieces),
        out_specs=hbm,
        out_shape=jax.ShapeDtypeStruct((rows, width), bf16),
        scratch_shapes=[pltpu.SemaphoreType.DMA((len(pieces),))],
        compiler_params=room(6),
        cost_estimate=cost(1 << 28),
        name="place",
    )(scalar(core), *pieces)


def local(tokens, forget, attn_gain, projections, out_weight, ffn_gain, expand_weight, down_weight):
    row_count, width = tokens.shape
    head_count = forget.shape[1]
    head_size = projections.shape[2] // head_count
    chips = lax.axis_size("tp") // cores
    core = lax.axis_index("tp") % cores
    parity = lax.axis_index("seq") % 2

    far = [across_chips(x) for x in cut_columns(parity, out_weight, 2)]
    out_partner = swap_cores(out_weight)
    expand_other = swap_cores(expand_weight)
    down_other = swap_cores(down_weight)

    k, v, normed, query_weight, column, row, state, sent = project(
        tokens, attn_gain, forget, projections, head_size
    )
    before = incoming_state(state, sent, head_size)
    q = queries(normed, query_weight, head_size)
    parts = 2
    inside = []
    for part in range(parts):
        inside.append(block_attention(q, k, v, column, row, head_size, part, parts))
    kept = finish_heads(core, q, column, before, inside, head_size)
    given = finish_heads(1 - core, q, column, before, inside, head_size)
    moved = swap_cores(given)
    sums, expand_here, expand_other = project_own_heads(
        kept, moved, out_weight, out_partner, expand_weight, expand_other
    )
    for hop in range(1, chips):
        other = [with_seq(x, 1) for x in far]
        weights = [x for value in far + other for x in (value, swap_cores(value))]
        kept, moved = across_chips(kept), across_chips(moved)
        sums = project_far_heads(parity, kept, moved, weights, sums)
        if hop + 1 < chips:
            far = [across_chips(x) for x in far]
    residual, normed_ffn = add_residual(core, tokens, sums, ffn_gain)
    hidden, down_here, down_other = expand(normed_ffn, expand_here, expand_other, down_weight, down_other)
    pieces = 4
    span = width // pieces
    mine, theirs = [], []
    for piece in range(pieces):
        partial = down(hidden, down_here, down_other, piece * span, span)
        moving, others = partial, []
        for _ in range(1, chips):
            moving = across_chips(moving)
            others.append(moving)
        mine.append(add_partials(piece * span, residual, partial, others))
        theirs.append(swap_cores(mine[-1]))
    return place(core, mine, theirs, row_count)


def solution(mesh):
    placed = (
        P("seq", None),
        P("seq", "tp"),
        P(),
        P(None, None, "tp"),
        P("tp", None),
        P(),
        P(None, None, "tp"),
        P("tp", None),
    )
    return jax.shard_map(
        local, mesh=mesh, in_specs=placed, out_specs=P("seq", None), check_vma=False
    )
```

time: 236 us -> 140 us (0.59)
  waiting for transfers between devices: 139 us -> 70.1 us
  matrix products: 39.8 us -> 0 us
  Pallas kernels: 0 us -> 29.2 us
  blocking collectives: 22.3 us -> 0 us
  starting transfers between devices: 0.35 us -> 22.4 us
  other arithmetic: 16.5 us -> 0 us
  local copies, waits for them, and re-layouts: 3.6 us -> 16.8 us
  between operations: 13.3 us -> 0.48 us
    reduce_scatter x2 -> x0, waiting for transfers between devices: 74.5 us -> none  [the longest x1 43.2 us: local(): lax.psum_scatter(jnp.dot(picked, out_weight, preferred_element_type=jnp.f...]
    ppermute x0 -> x25, waiting for transfers between devices: none -> 70.1 us  [the longest x8 48.9 us: across_chips(): lax.ppermute(value, 'tp', [(i, (i + cores) % count) for i in range(count)])]
    all_gather x3 -> x0, waiting for transfers between devices: 64.3 us -> none  [the longest x1 22.7 us: local(): return lax.all_gather(own_output, 'tp', axis=0, tiled=True)]
    dot_general x9 -> x0, matrix products: 39.8 us -> none  [the longest x3 11.4 us: local(): jnp.dot(normed, projections[which], preferred_element_type=jnp.float32)]
    pallas_call x0 -> x23, Pallas kernels: none -> 29.2 us  [the longest x1 5.86 us: project(): pl.pallas_call(functools.partial(project_kernel, size), in_specs=[hbm, vm...]
    ppermute x0 -> x25, starting transfers between devices: none -> 22.4 us  [the longest x5 10.7 us: with_seq(): return lax.ppermute(value, 'seq', [(i, i ^ bit) for i in range(count)])]
    all_gather x1 -> x0, blocking collectives: 22.3 us -> none  [carried_in(): pieces = jax.tree.map(lambda part: lax.all_gather(part, axis), value)]
    unnamed x15 -> x32, local copies, waits for them, and re-layouts: 3.19 us -> 16.8 us
  transfers between devices with their start and end apart: 5 -> 25, of which waited for: 5 -> 14; matrix products, arithmetic and copies ran while one was open for 5% -> 0% of each run, Pallas kernels for 0% -> 15%
where the time goes in v1:
time: 140 us; the launch traced here: 139 us
  waiting for transfers between devices  70.1 us (50%)
  Pallas kernels  29.2 us (21%)
  starting transfers between devices  22.4 us (16%)
  local copies, waits for them, and re-layouts  16.8 us (12%)
    ppermute x8, waiting for transfers between devices, across_chips(): lax.ppermute(value, 'tp', [(i, (i + cores) % count) for i in range(count)])  48.9 us
    ppermute x5, waiting for transfers between devices, with_seq(): return lax.ppermute(value, 'seq', [(i, i ^ bit) for i in range(count)])  19.6 us
    unnamed x32, local copies, waits for them, and re-layouts  16.8 us
    ppermute x5, starting transfers between devices, with_seq(): return lax.ppermute(value, 'seq', [(i, i ^ bit) for i in range(count)])  10.7 us
    ppermute x8, starting transfers between devices, across_chips(): lax.ppermute(value, 'tp', [(i, (i + cores) % count) for i in range(count)])  9.77 us
    pallas_call x1, Pallas kernels, project(): pl.pallas_call(functools.partial(project_kernel, size), in_specs=[hbm, vm...  5.86 us
    pallas_call x1, Pallas kernels, expand(): pl.pallas_call(expand_kernel, in_specs=[vmem] * 3 + [hbm] * 2, out_specs=...  5.09 us
    pallas_call x1, Pallas kernels, project_own_heads(): pl.pallas_call(own_heads_kernel, in_specs=[vmem] * 2 + [hbm] * 4, out_spe...  4.33 us
  transfers between devices with their start and end apart: 25, of which 14 were waited for; matrix products, arithmetic and copies ran while one was open for 0% of the time, Pallas kernels for 15%

profile of v1, /device:TPU:0, one launch (start us, length us, event | category | flops | bytes accessed | tf_op | source)
XLA Modules:
  0.0 139.0 jit_solution(17896383313275729703)
XLA Ops:
  2.6 2.8 %copy-done.3 = bf16[3,2048,512]{2,1,0:T(8,128)(2,1)S(1)} copy-done((bf16[3,2048,512]{2,1,0:T(8,128)(2,1)S(1)}, bf16[3,2048,512]{2,1,0:T(8,128)(2,1)}, u32[]{:S(2)}) %copy-start.3) | copy-done | bytes 6291480
  6.8 5.9 %project.1 = (bf16[512,512]{1,0:T(8,128)(2,1)S(1)}, bf16[512,512]{1,0:T(8,128)(2,1)S(1)}, bf16[512,2048]{1,0:T(8,128)(2,1)S(1)}, bf16[2048,512]{1,0:T(8,128)(2,1...) custom-call(bf16[512,2048]{1,0:T(8,128)(2,1)S(1)} %copy-done, ...), custom_call_target="tpu_custom_call" | custom-call | flops 2147483648 | tf_op jit(solution)/shard_map/project/pallas_call | solution.py:177
  15.4 2.5 %collective-permute-start = (bf16[272,128]{1,0:T(8,128)(2,1)}, bf16[272,128]{1,0:T(8,128)(2,1)}, u32[]{:S(2)}, u32[]{:S(2)}) collective-permute-start(bf16[272,128]{1,0:T(8,128)(2,1)} %get-tuple-element.34), channel_id=1, source_target_pairs={{0,4},{4,0},{8,12},{12,8},{16,20},{20,16},{24,28},{28,24},{1,5},{5... | collective-permute-start | bytes 208904 | tf_op jit(solution)/shard_map/ppermute | solution.py:79
  22.0 1.9 %collective-permute-start.1 = (bf16[272,128]{1,0:T(8,128)(2,1)S(1)}, bf16[272,128]{1,0:T(8,128)(2,1)S(1)}, u32[]{:S(2)}, u32[]{:S(2)}) collective-permute-start(bf16[272,128]{1,0:T(8,128)(2,1)S(1)} %get-tuple-element.37), channel_id=1, source_target_pairs={{0,8},{4,12},{8,0},{12,4},{16,24},{20,28},{24,16},{28,20},{1,9},{5... | collective-permute-start | bytes 208904 | tf_op jit(solution)/shard_map/ppermute | solution.py:79
  26.4 2.9 %collective-permute-start.2 = (bf16[272,128]{1,0:T(8,128)(2,1)S(1)}, bf16[272,128]{1,0:T(8,128)(2,1)S(1)}, u32[]{:S(2)}, u32[]{:S(2)}) collective-permute-start(bf16[272,128]{1,0:T(8,128)(2,1)S(1)} %get-tuple-element.40), channel_id=1, source_target_pairs={{0,16},{4,20},{8,24},{12,28},{16,0},{20,4},{24,8},{28,12},{1,17},{... | collective-permute-start | bytes 208904 | tf_op jit(solution)/shard_map/ppermute | solution.py:79
  35.8 1.8 %collective-permute-start.3 = (bf16[256,512]{1,0:T(8,128)(2,1)S(1)}, bf16[256,512]{1,0:T(8,128)(2,1)S(1)}, u32[]{:S(2)}, u32[]{:S(2)}) collective-permute-start(bf16[256,512]{1,0:T(8,128)(2,1)S(1)} %finish_heads.2.kept), channel_id=1, source_target_pairs={{0,2},{1,3},{2,0},{3,1},{4,6},{5,7},{6,4},{7,5},{8,10},{9,11},{10,... | collective-permute-start | bytes 786440 | tf_op jit(solution)/shard_map/ppermute | solution.py:74
  37.9 7.1 %collective-permute-done.3.kept = bf16[256,512]{1,0:T(8,128)(2,1)S(1)} collective-permute-done((bf16[256,512]{1,0:T(8,128)(2,1)S(1)}, bf16[256,512]{1,0:T(8,128)(2,1)S(1)}, u32[]{:S(2)}, u32[]{:S(2)}) %collective-permute-start.3) | collective-permute-done | bytes 262176 | tf_op jit(solution)/shard_map/ppermute | solution.py:74
  46.8 9.5 %collective-permute-done.6.refs_0_ = bf16[512,512]{1,0:T(8,128)(2,1)S(1)} collective-permute-done((bf16[512,512]{1,0:T(8,128)(2,1)S(1)}, bf16[512,512]{1,0:T(8,128)(2,1)S(1)}, u32[]{:S(2)}, u32[]{:S(2)}) %collective-permute-start.6) | collective-permute-done | bytes 524320 | tf_op jit(solution)/shard_map/ppermute | solution.py:74
  56.3 1.7 %collective-permute-start.5 = (bf16[256,512]{1,0:T(8,128)(2,1)S(1)}, bf16[256,512]{1,0:T(8,128)(2,1)S(1)}, u32[]{:S(2)}, u32[]{:S(2)}) collective-permute-start(bf16[256,512]{1,0:T(8,128)(2,1)S(1)} %collective-permute-done.4.moved), channel_id=1, source_target_pairs={{0,2},{1,3},{2,0},{3,1},{4,6},{5,7},{6,4},{7,5},{8,10},{9,11},{10,... | collective-permute-start | bytes 786440 | tf_op jit(solution)/shard_map/ppermute | solution.py:74
  58.0 9.5 %collective-permute-done.8.refs_2_ = bf16[512,512]{1,0:T(8,128)(2,1)S(1)} collective-permute-done((bf16[512,512]{1,0:T(8,128)(2,1)S(1)}, bf16[512,512]{1,0:T(8,128)(2,1)S(1)}, u32[]{:S(2)}, u32[]{:S(2)}) %collective-permute-start.8) | collective-permute-done | bytes 524320 | tf_op jit(solution)/shard_map/ppermute | solution.py:74
  67.5 1.7 %collective-permute-start.10 = (bf16[512,512]{1,0:T(8,128)(2,1)S(1)}, bf16[512,512]{1,0:T(8,128)(2,1)S(1)}, u32[]{:S(2)}, u32[]{:S(2)}) collective-permute-start(bf16[512,512]{1,0:T(8,128)(2,1)S(1)} %collective-permute-done.6.refs_0_), channel_id=1, source_target_pairs={{0,4},{4,0},{8,12},{12,8},{16,20},{20,16},{24,28},{28,24},{1,5},{5... | collective-permute-start | bytes 1572872 | tf_op jit(solution)/shard_map/ppermute | solution.py:79
  69.3 3.4 %collective-permute-done.5.moved = bf16[256,512]{1,0:T(8,128)(2,1)S(1)} collective-permute-done((bf16[256,512]{1,0:T(8,128)(2,1)S(1)}, bf16[256,512]{1,0:T(8,128)(2,1)S(1)}, u32[]{:S(2)}, u32[]{:S(2)}) %collective-permute-start.5) | collective-permute-done | bytes 262176 | tf_op jit(solution)/shard_map/ppermute | solution.py:74
  72.7 1.8 %collective-permute-start.12 = (bf16[512,512]{1,0:T(8,128)(2,1)S(1)}, bf16[512,512]{1,0:T(8,128)(2,1)S(1)}, u32[]{:S(2)}, u32[]{:S(2)}) collective-permute-start(bf16[512,512]{1,0:T(8,128)(2,1)S(1)} %collective-permute-done.8.refs_2_), channel_id=1, source_target_pairs={{0,4},{4,0},{8,12},{12,8},{16,20},{20,16},{24,28},{28,24},{1,5},{5... | collective-permute-start | bytes 1572872 | tf_op jit(solution)/shard_map/ppermute | solution.py:79
  74.4 7.9 %collective-permute-done.10.refs_4_ = bf16[512,512]{1,0:T(8,128)(2,1)S(1)} collective-permute-done((bf16[512,512]{1,0:T(8,128)(2,1)S(1)}, bf16[512,512]{1,0:T(8,128)(2,1)S(1)}, u32[]{:S(2)}, u32[]{:S(2)}) %collective-permute-start.10) | collective-permute-done | bytes 524320 | tf_op jit(solution)/shard_map/ppermute | solution.py:79
  82.3 9.4 %collective-permute-done.12.refs_6_ = bf16[512,512]{1,0:T(8,128)(2,1)S(1)} collective-permute-done((bf16[512,512]{1,0:T(8,128)(2,1)S(1)}, bf16[512,512]{1,0:T(8,128)(2,1)S(1)}, u32[]{:S(2)}, u32[]{:S(2)}) %collective-permute-start.12) | collective-permute-done | bytes 524320 | tf_op jit(solution)/shard_map/ppermute | solution.py:79
  92.3 3.4 %copy-done.2 = bf16[2,2048,1024]{2,1,0:T(8,128)(2,1)S(1)} copy-done((bf16[2,2048,1024]{2,1,0:T(8,128)(2,1)S(1)}, bf16[2,2048,1024]{2,1,0:T(8,128)(2,1)}, u32[]{:S(2)}) %copy-start.2) | copy-done | bytes 8388632
  95.7 4.3 %project_own_heads.1 = (f32[256,2048]{1,0:T(8,128)S(1)}, bf16[2,2048,1024]{2,1,0:T(8,128)(2,1)S(1)}, bf16[2,2048,1024]{2,1,0:T(8,128)(2,1)S(1)}) custom-call(bf16[256,512]{1,0:T(8,128)(2,1)S(1)} %finish_heads.2.kept, bf16[256,512]{1,0:T(8,128)(2,1)S(1)} %collective-permute-done.4.moved, bf16[512,2048]{1,0:T(8,128)(2,1)S(1)} %copy-done.8, ...), custom_call_target="tpu_custom_call" | custom-call | flops 1073741824 | tf_op jit(solution)/shard_map/project_own_heads/pallas_call | solution.py:356
  103.7 5.1 %expand.1 = (bf16[256,2048]{1,0:T(8,128)(2,1)S(1)}, bf16[1024,2048]{1,0:T(8,128)(2,1)S(1)}, bf16[1024,2048]{1,0:T(8,128)(2,1)S(1)}) custom-call(bf16[256,2048]{1,0:T(8,128)(2,1)S(1)} %get-tuple-element.49.rows_in, bf16[2,2048,1024]{2,1,0:T(8,128)(2,1)S(1)} %get-tuple-element.50.own, bf16[2,2048,1024]{2,1,0:T(8,128)(2,1)S(1)} %get-tuple-element.51.other, ...), custom_call_target="tpu_custom_call" | custom-call | flops 4294967296 | tf_op jit(solution)/shard_map/expand/pallas_call | solution.py:436
  110.2 1.8 %collective-permute-start.23 = (bf16[256,512]{1,0:T(8,128)(2,1)S(1)}, bf16[256,512]{1,0:T(8,128)(2,1)S(1)}, u32[]{:S(2)}, u32[]{:S(2)}) collective-permute-start(bf16[256,512]{1,0:T(8,128)(2,1)S(1)} %shard_map.87.own), channel_id=1, source_target_pairs={{0,2},{1,3},{2,0},{3,1},{4,6},{5,7},{6,4},{7,5},{8,10},{9,11},{10,... | collective-permute-start | bytes 786440 | tf_op jit(solution)/shard_map/ppermute | solution.py:74
  113.0 1.8 %collective-permute-start.19 = (bf16[256,512]{1,0:T(8,128)(2,1)S(1)}, bf16[256,512]{1,0:T(8,128)(2,1)S(1)}, u32[]{:S(2)}, u32[]{:S(2)}) collective-permute-start(bf16[256,512]{1,0:T(8,128)(2,1)S(1)} %shard_map.85.own), channel_id=1, source_target_pairs={{0,2},{1,3},{2,0},{3,1},{4,6},{5,7},{6,4},{7,5},{8,10},{9,11},{10,... | collective-permute-start | bytes 786440 | tf_op jit(solution)/shard_map/ppermute | solution.py:74
  115.9 3.6 %collective-permute-done.23.refs_0_ = bf16[256,512]{1,0:T(8,128)(2,1)S(1)} collective-permute-done((bf16[256,512]{1,0:T(8,128)(2,1)S(1)}, bf16[256,512]{1,0:T(8,128)(2,1)S(1)}, u32[]{:S(2)}, u32[]{:S(2)}) %collective-permute-start.23) | collective-permute-done | bytes 262176 | tf_op jit(solution)/shard_map/ppermute | solution.py:74
  119.6 5.4 %collective-permute-done.21.refs_0_ = bf16[256,512]{1,0:T(8,128)(2,1)S(1)} collective-permute-done((bf16[256,512]{1,0:T(8,128)(2,1)S(1)}, bf16[256,512]{1,0:T(8,128)(2,1)S(1)}, u32[]{:S(2)}, u32[]{:S(2)}) %collective-permute-start.21) | collective-permute-done | bytes 262176 | tf_op jit(solution)/shard_map/ppermute | solution.py:74
  125.2 5.4 %collective-permute-done.19.refs_0_ = bf16[256,512]{1,0:T(8,128)(2,1)S(1)} collective-permute-done((bf16[256,512]{1,0:T(8,128)(2,1)S(1)}, bf16[256,512]{1,0:T(8,128)(2,1)S(1)}, u32[]{:S(2)}, u32[]{:S(2)}) %collective-permute-start.19) | collective-permute-done | bytes 262176 | tf_op jit(solution)/shard_map/ppermute | solution.py:74
  130.9 4.9 %collective-permute-done.17.refs_0_ = bf16[256,512]{1,0:T(8,128)(2,1)S(1)} collective-permute-done((bf16[256,512]{1,0:T(8,128)(2,1)S(1)}, bf16[256,512]{1,0:T(8,128)(2,1)S(1)}, u32[]{:S(2)}, u32[]{:S(2)}) %collective-permute-start.17) | collective-permute-done | bytes 262176 | tf_op jit(solution)/shard_map/ppermute | solution.py:74
  (81 shorter events, 33.1 us)
Async XLA Ops:
  0.0 92.3 %collective-permute-start.15 = (bf16[2,2048,1024]{2,1,0:T(8,128)(2,1)}, bf16[2,2048,1024]{2,1,0:T(8,128)(2,1)}, u32[]{:S(2)}, u32[]{:S(2)}) collective-permute-start(bf16[2,2048,1024]{2,1,0:T(8,128)(2,1)} %expand_own.1), channel_id=1, source_target_pairs={{0,1},{1,0},{2,3},{3,2},{4,5},{5,4},{6,7},{7,6},{8,9},{9,8},{10,11... | collective-permute-start | bytes 25165832 | tf_op jit(solution)/shard_map/ppermute | solution.py:69
  0.5 101.7 %collective-permute-start.16 = (bf16[1024,2048]{1,0:T(8,128)(2,1)}, bf16[1024,2048]{1,0:T(8,128)(2,1)}, u32[]{:S(2)}, u32[]{:S(2)}) collective-permute-start(bf16[1024,2048]{1,0:T(8,128)(2,1)} %down_own.1), channel_id=1, source_target_pairs={{0,1},{1,0},{2,3},{3,2},{4,5},{5,4},{6,7},{7,6},{8,9},{9,8},{10,11... | collective-permute-start | bytes 12582920 | tf_op jit(solution)/shard_map/ppermute | solution.py:69
  0.5 91.2 %collective-permute-start.14 = (bf16[512,2048]{1,0:T(8,128)(2,1)}, bf16[512,2048]{1,0:T(8,128)(2,1)}, u32[]{:S(2)}, u32[]{:S(2)}) collective-permute-start(bf16[512,2048]{1,0:T(8,128)(2,1)} %own.1), channel_id=1, source_target_pairs={{0,1},{1,0},{2,3},{3,2},{4,5},{5,4},{6,7},{7,6},{8,9},{9,8},{10,11... | collective-permute-start | bytes 6291464 | tf_op jit(solution)/shard_map/ppermute | solution.py:69
  15.4 5.7 %collective-permute-start = (bf16[272,128]{1,0:T(8,128)(2,1)}, bf16[272,128]{1,0:T(8,128)(2,1)}, u32[]{:S(2)}, u32[]{:S(2)}) collective-permute-start(bf16[272,128]{1,0:T(8,128)(2,1)} %get-tuple-element.34), channel_id=1, source_target_pairs={{0,4},{4,0},{8,12},{12,8},{16,20},{20,16},{24,28},{28,24},{1,5},{5... | collective-permute-start | bytes 208904 | tf_op jit(solution)/shard_map/ppermute | solution.py:79
  22.0 4.4 %collective-permute-start.1 = (bf16[272,128]{1,0:T(8,128)(2,1)S(1)}, bf16[272,128]{1,0:T(8,128)(2,1)S(1)}, u32[]{:S(2)}, u32[]{:S(2)}) collective-permute-start(bf16[272,128]{1,0:T(8,128)(2,1)S(1)} %get-tuple-element.37), channel_id=1, source_target_pairs={{0,8},{4,12},{8,0},{12,4},{16,24},{20,28},{24,16},{28,20},{1,9},{5... | collective-permute-start | bytes 208904 | tf_op jit(solution)/shard_map/ppermute | solution.py:79
  26.4 5.3 %collective-permute-start.2 = (bf16[272,128]{1,0:T(8,128)(2,1)S(1)}, bf16[272,128]{1,0:T(8,128)(2,1)S(1)}, u32[]{:S(2)}, u32[]{:S(2)}) collective-permute-start(bf16[272,128]{1,0:T(8,128)(2,1)S(1)} %get-tuple-element.40), channel_id=1, source_target_pairs={{0,16},{4,20},{8,24},{12,28},{16,0},{20,4},{24,8},{28,12},{1,17},{... | collective-permute-start | bytes 208904 | tf_op jit(solution)/shard_map/ppermute | solution.py:79
  33.2 4.4 %collective-permute-start.4 = (bf16[256,512]{1,0:T(8,128)(2,1)S(1)}, bf16[256,512]{1,0:T(8,128)(2,1)S(1)}, u32[]{:S(2)}, u32[]{:S(2)}) collective-permute-start(bf16[256,512]{1,0:T(8,128)(2,1)S(1)} %finish_heads.3), channel_id=1, source_target_pairs={{0,1},{1,0},{2,3},{3,2},{4,5},{5,4},{6,7},{7,6},{8,9},{9,8},{10,11... | collective-permute-start | bytes 786440 | tf_op jit(solution)/shard_map/ppermute | solution.py:69
  35.8 9.2 %collective-permute-start.3 = (bf16[256,512]{1,0:T(8,128)(2,1)S(1)}, bf16[256,512]{1,0:T(8,128)(2,1)S(1)}, u32[]{:S(2)}, u32[]{:S(2)}) collective-permute-start(bf16[256,512]{1,0:T(8,128)(2,1)S(1)} %finish_heads.2.kept), channel_id=1, source_target_pairs={{0,2},{1,3},{2,0},{3,1},{4,6},{5,7},{6,4},{7,5},{8,10},{9,11},{10,... | collective-permute-start | bytes 786440 | tf_op jit(solution)/shard_map/ppermute | solution.py:74
  37.6 18.7 %collective-permute-start.6 = (bf16[512,512]{1,0:T(8,128)(2,1)S(1)}, bf16[512,512]{1,0:T(8,128)(2,1)S(1)}, u32[]{:S(2)}, u32[]{:S(2)}) collective-permute-start(bf16[512,512]{1,0:T(8,128)(2,1)S(1)} %get-tuple-element.45), channel_id=1, source_target_pairs={{0,2},{1,3},{2,0},{3,1},{4,6},{5,7},{6,4},{7,5},{8,10},{9,11},{10,... | collective-permute-start | bytes 1572872 | tf_op jit(solution)/shard_map/ppermute | solution.py:74
  45.1 22.5 %collective-permute-start.8 = (bf16[512,512]{1,0:T(8,128)(2,1)S(1)}, bf16[512,512]{1,0:T(8,128)(2,1)S(1)}, u32[]{:S(2)}, u32[]{:S(2)}) collective-permute-start(bf16[512,512]{1,0:T(8,128)(2,1)S(1)} %get-tuple-element.46), channel_id=1, source_target_pairs={{0,2},{1,3},{2,0},{3,1},{4,6},{5,7},{6,4},{7,5},{8,10},{9,11},{10,... | collective-permute-start | bytes 1572872 | tf_op jit(solution)/shard_map/ppermute | solution.py:74
  56.3 16.4 %collective-permute-start.5 = (bf16[256,512]{1,0:T(8,128)(2,1)S(1)}, bf16[256,512]{1,0:T(8,128)(2,1)S(1)}, u32[]{:S(2)}, u32[]{:S(2)}) collective-permute-start(bf16[256,512]{1,0:T(8,128)(2,1)S(1)} %collective-permute-done.4.moved), channel_id=1, source_target_pairs={{0,2},{1,3},{2,0},{3,1},{4,6},{5,7},{6,4},{7,5},{8,10},{9,11},{10,... | collective-permute-start | bytes 786440 | tf_op jit(solution)/shard_map/ppermute | solution.py:74
  67.5 14.8 %collective-permute-start.10 = (bf16[512,512]{1,0:T(8,128)(2,1)S(1)}, bf16[512,512]{1,0:T(8,128)(2,1)S(1)}, u32[]{:S(2)}, u32[]{:S(2)}) collective-permute-start(bf16[512,512]{1,0:T(8,128)(2,1)S(1)} %collective-permute-done.6.refs_0_), channel_id=1, source_target_pairs={{0,4},{4,0},{8,12},{12,8},{16,20},{20,16},{24,28},{28,24},{1,5},{5... | collective-permute-start | bytes 1572872 | tf_op jit(solution)/shard_map/ppermute | solution.py:79
  72.7 19.1 %collective-permute-start.12 = (bf16[512,512]{1,0:T(8,128)(2,1)S(1)}, bf16[512,512]{1,0:T(8,128)(2,1)S(1)}, u32[]{:S(2)}, u32[]{:S(2)}) collective-permute-start(bf16[512,512]{1,0:T(8,128)(2,1)S(1)} %collective-permute-done.8.refs_2_), channel_id=1, source_target_pairs={{0,4},{4,0},{8,12},{12,8},{16,20},{20,16},{24,28},{28,24},{1,5},{5... | collective-permute-start | bytes 1572872 | tf_op jit(solution)/shard_map/ppermute | solution.py:79
  82.3 17.7 %collective-permute-start.7 = (bf16[512,512]{1,0:T(8,128)(2,1)S(1)}, bf16[512,512]{1,0:T(8,128)(2,1)S(1)}, u32[]{:S(2)}, u32[]{:S(2)}) collective-permute-start(bf16[512,512]{1,0:T(8,128)(2,1)S(1)} %collective-permute-done.6.refs_0_), channel_id=1, source_target_pairs={{0,1},{1,0},{2,3},{3,2},{4,5},{5,4},{6,7},{7,6},{8,9},{9,8},{10,11... | collective-permute-start | bytes 1572872 | tf_op jit(solution)/shard_map/ppermute | solution.py:69
  91.7 8.3 %collective-permute-start.9 = (bf16[512,512]{1,0:T(8,128)(2,1)S(1)}, bf16[512,512]{1,0:T(8,128)(2,1)S(1)}, u32[]{:S(2)}, u32[]{:S(2)}) collective-permute-start(bf16[512,512]{1,0:T(8,128)(2,1)S(1)} %collective-permute-done.8.refs_2_), channel_id=1, source_target_pairs={{0,1},{1,0},{2,3},{3,2},{4,5},{5,4},{6,7},{7,6},{8,9},{9,8},{10,11... | collective-permute-start | bytes 1572872 | tf_op jit(solution)/shard_map/ppermute | solution.py:69
  91.8 8.3 %collective-permute-start.11 = (bf16[512,512]{1,0:T(8,128)(2,1)S(1)}, bf16[512,512]{1,0:T(8,128)(2,1)S(1)}, u32[]{:S(2)}, u32[]{:S(2)}) collective-permute-start(bf16[512,512]{1,0:T(8,128)(2,1)S(1)} %collective-permute-done.10.refs_4_), channel_id=1, source_target_pairs={{0,1},{1,0},{2,3},{3,2},{4,5},{5,4},{6,7},{7,6},{8,9},{9,8},{10,11... | collective-permute-start | bytes 1572872 | tf_op jit(solution)/shard_map/ppermute | solution.py:69
  92.3 7.8 %collective-permute-start.13 = (bf16[512,512]{1,0:T(8,128)(2,1)S(1)}, bf16[512,512]{1,0:T(8,128)(2,1)S(1)}, u32[]{:S(2)}, u32[]{:S(2)}) collective-permute-start(bf16[512,512]{1,0:T(8,128)(2,1)S(1)} %collective-permute-done.12.refs_6_), channel_id=1, source_target_pairs={{0,1},{1,0},{2,3},{3,2},{4,5},{5,4},{6,7},{7,6},{8,9},{9,8},{10,11... | collective-permute-start | bytes 1572872 | tf_op jit(solution)/shard_map/ppermute | solution.py:69
  110.2 9.2 %collective-permute-start.23 = (bf16[256,512]{1,0:T(8,128)(2,1)S(1)}, bf16[256,512]{1,0:T(8,128)(2,1)S(1)}, u32[]{:S(2)}, u32[]{:S(2)}) collective-permute-start(bf16[256,512]{1,0:T(8,128)(2,1)S(1)} %shard_map.87.own), channel_id=1, source_target_pairs={{0,2},{1,3},{2,0},{3,1},{4,6},{5,7},{6,4},{7,5},{8,10},{9,11},{10,... | collective-permute-start | bytes 786440 | tf_op jit(solution)/shard_map/ppermute | solution.py:74
  112.0 13.1 %collective-permute-start.21 = (bf16[256,512]{1,0:T(8,128)(2,1)S(1)}, bf16[256,512]{1,0:T(8,128)(2,1)S(1)}, u32[]{:S(2)}, u32[]{:S(2)}) collective-permute-start(bf16[256,512]{1,0:T(8,128)(2,1)S(1)} %shard_map.86.own), channel_id=1, source_target_pairs={{0,2},{1,3},{2,0},{3,1},{4,6},{5,7},{6,4},{7,5},{8,10},{9,11},{10,... | collective-permute-start | bytes 786440 | tf_op jit(solution)/shard_map/ppermute | solution.py:74
  113.0 17.7 %collective-permute-start.19 = (bf16[256,512]{1,0:T(8,128)(2,1)S(1)}, bf16[256,512]{1,0:T(8,128)(2,1)S(1)}, u32[]{:S(2)}, u32[]{:S(2)}) collective-permute-start(bf16[256,512]{1,0:T(8,128)(2,1)S(1)} %shard_map.85.own), channel_id=1, source_target_pairs={{0,2},{1,3},{2,0},{3,1},{4,6},{5,7},{6,4},{7,5},{8,10},{9,11},{10,... | collective-permute-start | bytes 786440 | tf_op jit(solution)/shard_map/ppermute | solution.py:74
  115.5 20.3 %collective-permute-start.17 = (bf16[256,512]{1,0:T(8,128)(2,1)S(1)}, bf16[256,512]{1,0:T(8,128)(2,1)S(1)}, u32[]{:S(2)}, u32[]{:S(2)}) collective-permute-start(bf16[256,512]{1,0:T(8,128)(2,1)S(1)} %shard_map.84.own), channel_id=1, source_target_pairs={{0,2},{1,3},{2,0},{3,1},{4,6},{5,7},{6,4},{7,5},{8,10},{9,11},{10,... | collective-permute-start | bytes 786440 | tf_op jit(solution)/shard_map/ppermute | solution.py:74
  119.5 16.4 %collective-permute-start.24 = (bf16[256,512]{1,0:T(8,128)(2,1)S(1)}, bf16[256,512]{1,0:T(8,128)(2,1)S(1)}, u32[]{:S(2)}, u32[]{:S(2)}) collective-permute-start(bf16[256,512]{1,0:T(8,128)(2,1)S(1)} %add_partials.7.refs_6_), channel_id=1, source_target_pairs={{0,1},{1,0},{2,3},{3,2},{4,5},{5,4},{6,7},{7,6},{8,9},{9,8},{10,11... | collective-permute-start | bytes 786440 | tf_op jit(solution)/shard_map/ppermute | solution.py:69
  125.2 10.8 %collective-permute-start.22 = (bf16[256,512]{1,0:T(8,128)(2,1)S(1)}, bf16[256,512]{1,0:T(8,128)(2,1)S(1)}, u32[]{:S(2)}, u32[]{:S(2)}) collective-permute-start(bf16[256,512]{1,0:T(8,128)(2,1)S(1)} %add_partials.6.refs_4_), channel_id=1, source_target_pairs={{0,1},{1,0},{2,3},{3,2},{4,5},{5,4},{6,7},{7,6},{8,9},{9,8},{10,11... | collective-permute-start | bytes 786440 | tf_op jit(solution)/shard_map/ppermute | solution.py:69
  130.8 5.2 %collective-permute-start.20 = (bf16[256,512]{1,0:T(8,128)(2,1)S(1)}, bf16[256,512]{1,0:T(8,128)(2,1)S(1)}, u32[]{:S(2)}, u32[]{:S(2)}) collective-permute-start(bf16[256,512]{1,0:T(8,128)(2,1)S(1)} %add_partials.5.refs_2_), channel_id=1, source_target_pairs={{0,1},{1,0},{2,3},{3,2},{4,5},{5,4},{6,7},{7,6},{8,9},{9,8},{10,11... | collective-permute-start | bytes 786440 | tf_op jit(solution)/shard_map/ppermute | solution.py:69
  (17 other events, 88.3 us)

commit v2 on v1

--- a/solution.py
+++ b/solution.py
@@ -14,10 +14,11 @@
 log2e = 1.4426950408889634
 
 f32, bf16 = jnp.float32, jnp.bfloat16
+chunks = 2
+spans = ((1,), (2, 4, 4))
 
 
 vmem = pl.BlockSpec(memory_space=pltpu.VMEM)
-smem = pl.BlockSpec(memory_space=pltpu.SMEM)
 hbm = pl.BlockSpec(memory_space=pltpu.HBM)
 
 
@@ -29,8 +30,8 @@
     return pltpu.CompilerParams(vmem_limit_bytes=mebibytes << 20)
 
 
-def scalar(value):
-    return value.astype(jnp.int32).reshape(1)
+def own_core():
+    return lax.axis_index("tp") % cores
 
 
 def iota(shape, axis):
@@ -77,33 +78,6 @@
 def with_seq(value, bit):
     count = lax.axis_size("seq")
     return lax.ppermute(value, "seq", [(i, i ^ bit) for i in range(count)])
-
-
-def cut_kernel(group, source, *refs):
-    outs, sems = refs[:-1], refs[-1]
-    share = outs[0].shape[1]
-    loads = []
-    for at, out in enumerate(outs):
-        columns = pl.ds(pl.multiple_of((len(outs) * group[0] + at) * share, share), share)
-        loads.append(pltpu.make_async_copy(source.at[:, columns], out, sems.at[at]))
-    for load in loads:
-        load.start()
-    for load in loads:
-        load.wait()
-
-
-def cut_columns(group, weight, pieces):
-    share = weight.shape[1] // (2 * pieces)
-    return pl.pallas_call(
-        cut_kernel,
-        in_specs=[smem, hbm],
-        out_specs=[hbm] * pieces,
-        out_shape=[jax.ShapeDtypeStruct((weight.shape[0], share), weight.dtype)] * pieces,
-        scratch_shapes=[pltpu.SemaphoreType.DMA((pieces,))],
-        compiler_params=room(1),
-        cost_estimate=cost(1 << 30),
-        name="cut_columns",
-    )(scalar(group), weight)
 
 
 def project_kernel(
@@ -185,7 +159,7 @@
             pltpu.SemaphoreType.DMA((7,)),
         ],
         cost_estimate=cost(4 * rows * width * mine),
-        compiler_params=room(24),
+        compiler_params=room(42),
         name="project",
     )(tokens, gain.reshape(1, width), forget.T, projections)
 
@@ -250,10 +224,10 @@
     )(q, k, v, column, row)
 
 
-def combine_kernel(first, size, later, state, before, got, new_state, new_before, sent):
+def combine_kernel(bit, size, state, before, got, new_before, *carried):
     tail = 16
     body, lanes = state.shape[0] - tail, state.shape[1]
-    is_later = later[0] != 0
+    is_later, first = (lax.axis_index("seq") & bit) != 0, bit == 1
     rest = pl.ds(body, tail)
     mine_decay, got_decay = state[rest, :], got[rest, :].astype(f32)
     early_decay = jnp.ones((tail, lanes), f32) if first else before[rest, :]
@@ -262,48 +236,48 @@
         theirs, own = got[at, :].astype(f32), state[at, :]
         prior = jnp.zeros((size, lanes), f32) if first else before[at, :]
         d_mine, d_got, d_early = (x[pair : pair + 1] for x in (mine_decay, got_decay, early_decay))
-        fresh = jnp.where(is_later, d_mine * theirs + own, d_got * own + theirs)
-        new_state[at, :] = fresh
-        sent[at, :] = fresh.astype(bf16)
+        if carried:
+            fresh = jnp.where(is_later, d_mine * theirs + own, d_got * own + theirs)
+            for ref in carried:
+                ref[at, :] = fresh.astype(ref.dtype)
         new_before[at, :] = jnp.where(is_later, prior + d_early * theirs, prior)
     decay = mine_decay * got_decay
-    new_state[rest, :] = decay
-    sent[rest, :] = decay.astype(bf16)
+    for ref in carried:
+        ref[rest, :] = decay.astype(ref.dtype)
     new_before[rest, :] = jnp.where(is_later, early_decay * got_decay, early_decay)
 
 
-def combine(first, size, later, state, before, got):
-    shape = state.shape
-    return pl.pallas_call(
-        functools.partial(combine_kernel, first, size),
-        in_specs=[smem] + [vmem] * 3,
-        out_specs=[vmem] * 3,
-        out_shape=[
-            jax.ShapeDtypeStruct(shape, f32),
-            jax.ShapeDtypeStruct(shape, f32),
-            jax.ShapeDtypeStruct(shape, bf16),
-        ],
+def combine(bit, size, last, state, before, got):
+    kinds = (f32,) if last else (f32, f32, bf16)
+    return pl.pallas_call(
+        functools.partial(combine_kernel, bit, size),
+        in_specs=[vmem] * 3,
+        out_specs=[vmem] * len(kinds),
+        out_shape=[jax.ShapeDtypeStruct(state.shape, kind) for kind in kinds],
         compiler_params=room(2),
         cost_estimate=cost(1 << 28),
         name="combine",
-    )(scalar(later), state, before, got)
+    )(state, before, got)
 
 
 def incoming_state(state, sent, size):
-    count, mine = lax.axis_size("seq"), lax.axis_index("seq")
+    count = lax.axis_size("seq")
     before, bit = state, 1
     while bit < count:
         got = with_seq(sent, bit)
-        state, before, sent = combine(bit == 1, size, mine & bit, state, before, got)
+        before, *carried = combine(bit, size, 2 * bit >= count, state, before, got)
+        if carried:
+            state, sent = carried
         bit *= 2
     return before
 
 
-def heads_kernel(size, parts, half, q, column, before, *refs):
+def heads_kernel(size, parts, side, start, q, column, before, *refs):
     locals_, out = refs[:parts], refs[parts]
     span, lanes = out.shape[0], 2 * size
     width = q.shape[1] // parts
-    here = pl.ds(pl.multiple_of(half[0] * span, span), span)
+    core = own_core() if side == 0 else 1 - own_core()
+    here = pl.ds(pl.multiple_of(core * (q.shape[0] // cores) + start, span), span)
     ones = (iota((lanes, lanes), 0) // size == iota((lanes, lanes), 1) // size).astype(bf16)
     first = iota((size, lanes), 1) < size
     growth = jnp.exp2(spread_heads(column[here, :], size))
@@ -323,99 +297,61 @@
         out[:, cut] = (attended * lax.rsqrt(mean_square + head_epsilon)).astype(bf16)
 
 
-def finish_heads(half, q, column, before, local_parts, size):
-    rows, mine = q.shape
-    span = rows // cores
-    return pl.pallas_call(
-        functools.partial(heads_kernel, size, len(local_parts)),
-        in_specs=[smem] + [vmem] * (3 + len(local_parts)),
+def finish_heads(side, start, span, q, column, before, local_parts, size):
+    mine = q.shape[1]
+    return pl.pallas_call(
+        functools.partial(heads_kernel, size, len(local_parts), side, start),
+        in_specs=[vmem] * (3 + len(local_parts)),
         out_specs=vmem,
         out_shape=jax.ShapeDtypeStruct((span, mine), bf16),
         cost_estimate=cost(span * mine * 2048),
         compiler_params=room(6),
         name="finish_heads",
-    )(scalar(half), q, column, before, *local_parts)
-
-
-def own_heads_kernel(kept, moved, own, partner, expand_own, expand_other, out, own_here, other_here, first, second, sems):
-    pairs = ((own, first), (partner, second), (expand_own, own_here), (expand_other, other_here))
-    loads = [pltpu.make_async_copy(a, b, sems.at[at]) for at, (a, b) in enumerate(pairs)]
-    for load in loads:
-        load.start()
-    for load in loads[:2]:
-        load.wait()
-    out[...] = dot(kept[...], first[...]) + dot(moved[...], second[...])
-    for load in loads[2:]:
-        load.wait()
-
-
-def project_own_heads(kept, moved, own, partner, expand_own, expand_other):
-    rows, depth = kept.shape
-    width = own.shape[1]
-    staged = jax.ShapeDtypeStruct(expand_own.shape, bf16)
+    )(q, column, before, *local_parts)
+
+
+def own_heads_kernel(kept, moved, own, partner, out):
+    out[...] = (dot(kept[...], own[...]) + dot(moved[...], partner[...])).astype(bf16)
+
+
+def project_heads(kept, moved, own, partner):
+    rows, (depth, width) = kept.shape[0], own.shape
     return pl.pallas_call(
         own_heads_kernel,
-        in_specs=[vmem] * 2 + [hbm] * 4,
-        out_specs=[vmem] * 3,
-        out_shape=[jax.ShapeDtypeStruct((rows, width), f32), staged, staged],
-        scratch_shapes=[pltpu.VMEM(own.shape, bf16), pltpu.VMEM(own.shape, bf16), pltpu.SemaphoreType.DMA((4,))],
+        in_specs=[vmem] * 4,
+        out_specs=vmem,
+        out_shape=jax.ShapeDtypeStruct((rows, width), bf16),
         cost_estimate=cost(4 * rows * depth * width),
         compiler_params=room(8),
-        name="project_own_heads",
-    )(kept, moved, own, partner, expand_own, expand_other)
-
-
-def far_heads_kernel(parity, kept, moved, *refs):
-    weights, (sums, out) = refs[:8], refs[8:]
-    share = weights[0].shape[1]
-    for at in range(4):
-        group = parity[0] if at < 2 else 1 - parity[0]
-        here = pl.ds(pl.multiple_of((2 * group + at % 2) * share, share), share)
-        part = dot(kept[...], weights[2 * at][...]) + dot(moved[...], weights[2 * at + 1][...])
-        out[:, here] = sums[:, here] + part
-
-
-def project_far_heads(parity, kept, moved, weights, sums):
-    rows, depth = kept.shape
-    width = sums.shape[1]
-    return pl.pallas_call(
-        far_heads_kernel,
-        in_specs=[smem] + [vmem] * 11,
-        out_specs=vmem,
-        out_shape=jax.ShapeDtypeStruct(sums.shape, f32),
-        input_output_aliases={11: 0},
-        cost_estimate=cost(4 * rows * depth * width),
-        compiler_params=room(12),
-        name="project_far_heads",
-    )(scalar(parity), kept, moved, *weights, sums)
-
-
-def residual_kernel(core, tok, sums, gain, residual, normed):
-    rows = sums.shape[0]
-    here = pl.ds(pl.multiple_of(core[0] * rows, rows), rows)
-    total = (tok[here, :].astype(f32) + sums[...]).astype(bf16)
+        name="project_heads",
+    )(kept, moved, own, partner)
+
+
+def residual_kernel(start, half, tok, gain, own, *refs):
+    others, residual, normed = refs[:-2], refs[-2], refs[-1]
+    rows = own.shape[0]
+    total = own[...].astype(f32)
+    for other in others:
+        total = total + other[...].astype(f32)
+    here = pl.ds(pl.multiple_of(own_core() * half + start, rows), rows)
+    total = (tok[here, :].astype(f32) + total).astype(bf16)
     residual[...] = total
     normed[...] = normalize(total.astype(f32), gain[...])
 
 
-def add_residual(core, tokens, sums, gain):
-    shape = jax.ShapeDtypeStruct(sums.shape, bf16)
-    return pl.pallas_call(
-        residual_kernel,
-        in_specs=[smem] + [vmem] * 3,
+def add_residual(tokens, gain, own, others, start):
+    shape = jax.ShapeDtypeStruct(own.shape, bf16)
+    return pl.pallas_call(
+        functools.partial(residual_kernel, start, tokens.shape[0] // cores),
+        in_specs=[vmem] * (3 + len(others)),
         out_specs=[vmem] * 2,
         out_shape=[shape, shape],
-        cost_estimate=cost(sums.size * 1024),
-        compiler_params=room(10),
-        name="add_residual",
-    )(scalar(core), tokens, sums, gain.reshape(1, -1))
-
-
-def expand_kernel(rows_in, own, other, down_own, down_other, out, own_here, other_here, sems):
-    pairs = ((down_own, own_here), (down_other, other_here))
-    loads = [pltpu.make_async_copy(a, b, sems.at[at]) for at, (a, b) in enumerate(pairs)]
-    for load in loads:
-        load.start()
+        cost_estimate=cost(own.size * 1024),
+        compiler_params=room(8),
+    )(tokens, gain.reshape(1, -1), own, *others)
+
+
+def expand_kernel(rows_in, own, other, out):
     hidden = own.shape[2]
     wide = hidden // 2
     for place, weight in enumerate((own, other)):
@@ -425,24 +361,20 @@
             half_gate = 0.5 * gate
             silu = half_gate * jnp.tanh(half_gate) + half_gate
             out[:, pl.ds(place * hidden + at, wide)] = (silu * up).astype(bf16)
-    for load in loads:
-        load.wait()
-
-
-def expand(rows_in, own, other, down_own, down_other):
+
+
+def expand(rows_in, own, other):
     rows, width = rows_in.shape
     hidden = own.shape[2]
-    staged = jax.ShapeDtypeStruct(down_own.shape, bf16)
     return pl.pallas_call(
         expand_kernel,
-        in_specs=[vmem] * 3 + [hbm] * 2,
-        out_specs=[vmem] * 3,
-        out_shape=[jax.ShapeDtypeStruct((rows, 2 * hidden), bf16), staged, staged],
-        scratch_shapes=[pltpu.SemaphoreType.DMA((2,))],
+        in_specs=[vmem] * 3,
+        out_specs=vmem,
+        out_shape=jax.ShapeDtypeStruct((rows, 2 * hidden), bf16),
         cost_estimate=cost(8 * rows * width * hidden),
-        compiler_params=room(8),
+        compiler_params=room(10),
         name="expand",
-    )(rows_in, own, other, down_own, down_other)
+    )(rows_in, own, other)
 
 
 def down_kernel(start, hidden, own, other, out):
@@ -483,36 +415,36 @@
     )(residual, own, *others)
 
 
-def place_kernel(count, core, *refs):
-    pieces, out, sems = refs[: 2 * count], refs[-2], refs[-1]
-    rows = pieces[0].shape[0]
-    loads, start = [], 0
-    for at in range(count):
-        span = pieces[2 * at].shape[1]
+def place_kernel(spots, half, *refs):
+    pieces, out, sems = refs[: 2 * len(spots)], refs[-2], refs[-1]
+    loads = []
+    for at, (row, column) in enumerate(spots):
+        rows, columns = pieces[2 * at].shape
         for side in range(2):
-            here = pl.ds(pl.multiple_of((core[0] if side == 0 else 1 - core[0]) * rows, rows), rows)
-            to = out.at[here, pl.ds(start, span)]
+            core = own_core() if side == 0 else 1 - own_core()
+            here = pl.ds(pl.multiple_of(core * half + row, rows), rows)
+            to = out.at[here, pl.ds(column, columns)]
             loads.append(pltpu.make_async_copy(pieces[2 * at + side], to, sems.at[2 * at + side]))
-        start += span
     for load in loads:
         load.start()
     for load in loads:
         load.wait()
 
 
-def place(core, mine, theirs, rows):
+def place(mine, theirs, spots, shape, target=None):
     pieces = [x for pair in zip(mine, theirs) for x in pair]
-    width = sum(x.shape[1] for x in mine)
-    return pl.pallas_call(
-        functools.partial(place_kernel, len(mine)),
-        in_specs=[smem] + [vmem] * len(pieces),
+    given = [] if target is None else [target]
+    return pl.pallas_call(
+        functools.partial(place_kernel, spots, shape[0] // cores),
+        in_specs=[vmem] * len(pieces) + [hbm] * len(given),
         out_specs=hbm,
-        out_shape=jax.ShapeDtypeStruct((rows, width), bf16),
+        out_shape=jax.ShapeDtypeStruct(shape, bf16),
+        input_output_aliases={len(pieces): 0} if given else {},
         scratch_shapes=[pltpu.SemaphoreType.DMA((len(pieces),))],
         compiler_params=room(6),
         cost_estimate=cost(1 << 28),
         name="place",
-    )(scalar(core), *pieces)
+    )(*pieces, *given)
 
 
 def local(tokens, forget, attn_gain, projections, out_weight, ffn_gain, expand_weight, down_weight):
@@ -520,12 +452,10 @@
     head_count = forget.shape[1]
     head_size = projections.shape[2] // head_count
     chips = lax.axis_size("tp") // cores
-    core = lax.axis_index("tp") % cores
-    parity = lax.axis_index("seq") % 2
-
-    far = [across_chips(x) for x in cut_columns(parity, out_weight, 2)]
+
+    half = row_count // cores
+    expand_other = swap_cores(expand_weight)
     out_partner = swap_cores(out_weight)
-    expand_other = swap_cores(expand_weight)
     down_other = swap_cores(down_weight)
 
     k, v, normed, query_weight, column, row, state, sent = project(
@@ -537,33 +467,37 @@
     inside = []
     for part in range(parts):
         inside.append(block_attention(q, k, v, column, row, head_size, part, parts))
-    kept = finish_heads(core, q, column, before, inside, head_size)
-    given = finish_heads(1 - core, q, column, before, inside, head_size)
-    moved = swap_cores(given)
-    sums, expand_here, expand_other = project_own_heads(
-        kept, moved, out_weight, out_partner, expand_weight, expand_other
-    )
-    for hop in range(1, chips):
-        other = [with_seq(x, 1) for x in far]
-        weights = [x for value in far + other for x in (value, swap_cores(value))]
-        kept, moved = across_chips(kept), across_chips(moved)
-        sums = project_far_heads(parity, kept, moved, weights, sums)
-        if hop + 1 < chips:
-            far = [across_chips(x) for x in far]
-    residual, normed_ffn = add_residual(core, tokens, sums, ffn_gain)
-    hidden, down_here, down_other = expand(normed_ffn, expand_here, expand_other, down_weight, down_other)
-    pieces = 4
-    span = width // pieces
-    mine, theirs = [], []
-    for piece in range(pieces):
-        partial = down(hidden, down_here, down_other, piece * span, span)
-        moving, others = partial, []
+    def exchanged(value):
+        others = []
         for _ in range(1, chips):
-            moving = across_chips(moving)
-            others.append(moving)
-        mine.append(add_partials(piece * span, residual, partial, others))
-        theirs.append(swap_cores(mine[-1]))
-    return place(core, mine, theirs, row_count)
+            value = across_chips(value)
+            others.append(value)
+        return others
+
+    chunk = half // chunks
+    sums = []
+    for at in range(chunks):
+        given = finish_heads(1, at * chunk, chunk, q, column, before, inside, head_size)
+        kept = finish_heads(0, at * chunk, chunk, q, column, before, inside, head_size)
+        moved = swap_cores(given)
+        part = project_heads(kept, moved, out_weight, out_partner)
+        sums.append((part, exchanged(part)))
+    mine, theirs, spots = [], [], []
+    for at, (part, others) in enumerate(sums):
+        residual, normed_ffn = add_residual(tokens, ffn_gain, part, others, at * chunk)
+        hidden = expand(normed_ffn, expand_weight, expand_other)
+        start = 0
+        for parts_of in spans[at]:
+            span = width // parts_of
+            partial = down(hidden, down_weight, down_other, start, span)
+            others = exchanged(partial)
+            mine.append(add_partials(start, residual, partial, others))
+            theirs.append(swap_cores(mine[-1]))
+            spots.append((at * chunk, start))
+            start += span
+    late = 2
+    output = place(mine[:-late], theirs[:-late], spots[:-late], tokens.shape)
+    return place(mine[-late:], theirs[-late:], spots[-late:], tokens.shape, output)
 
 
 def solution(mesh):

time: 140 us -> 79.2 us (0.57)
  waiting for transfers between devices: 70.1 us -> 32.9 us
  local copies, waits for them, and re-layouts: 16.8 us -> 3.03 us
  Pallas kernels: 29.2 us -> 24.3 us
  starting transfers between devices: 22.4 us -> 18.1 us
    ppermute x8 -> x6, waiting for transfers between devices: 48.9 us -> 27.7 us  [across_chips(): lax.ppermute(value, 'tp', [(i, (i + cores) % count) for i in range(count)])]
    ppermute x5 -> x3, waiting for transfers between devices: 19.6 us -> 3.56 us  [with_seq(): return lax.ppermute(value, 'seq', [(i, i ^ bit) for i in range(count)])]
    unnamed x32 -> x16, local copies, waits for them, and re-layouts: 16.8 us -> 3.03 us
    pallas_call x11 -> x15, Pallas kernels: 16 us -> 12 us  [the longest x2 5.23 us: expand(): pl.pallas_call(expand_kernel, in_specs=[vmem] * 3, out_specs=vmem, out_sh...]
    ppermute x5 -> x3, starting transfers between devices: 10.7 us -> 7.31 us  [with_seq(): return lax.ppermute(value, 'seq', [(i, i ^ bit) for i in range(count)])]
    ppermute x8 -> x6, starting transfers between devices: 9.77 us -> 9.15 us  [across_chips(): lax.ppermute(value, 'tp', [(i, (i + cores) % count) for i in range(count)])]
  transfers between devices with their start and end apart: 25 -> 18, of which waited for: 14 -> 11; matrix products, arithmetic and copies ran while one was open for 0% -> 0% of each run, Pallas kernels for 15% -> 30%
where the time goes in v2:
time: 79.2 us; the launch traced here: 78.8 us
  waiting for transfers between devices  32.9 us (42%)
  Pallas kernels  24.3 us (31%)
  starting transfers between devices  18.1 us (23%)
  local copies, waits for them, and re-layouts  3.03 us (4%)
    ppermute x6, waiting for transfers between devices, across_chips(): lax.ppermute(value, 'tp', [(i, (i + cores) % count) for i in range(count)])  27.7 us
    ppermute x6, starting transfers between devices, across_chips(): lax.ppermute(value, 'tp', [(i, (i + cores) % count) for i in range(count)])  9.15 us
    ppermute x3, starting transfers between devices, with_seq(): return lax.ppermute(value, 'seq', [(i, i ^ bit) for i in range(count)])  7.31 us
    pallas_call x2, Pallas kernels, expand(): pl.pallas_call(expand_kernel, in_specs=[vmem] * 3, out_specs=vmem, out_sh...  5.23 us
    pallas_call x1, Pallas kernels, project(): pl.pallas_call(functools.partial(project_kernel, size), in_specs=[hbm, vm...  4.81 us
    ppermute x3, waiting for transfers between devices, with_seq(): return lax.ppermute(value, 'seq', [(i, i ^ bit) for i in range(count)])  3.56 us
    unnamed x16, local copies, waits for them, and re-layouts  3.03 us
    pallas_call x4, Pallas kernels, down(): pl.pallas_call(functools.partial(down_kernel, start), in_specs=[vmem] * 3...  2.94 us
  transfers between devices with their start and end apart: 18, of which 11 were waited for; matrix products, arithmetic and copies ran while one was open for 0% of the time, Pallas kernels for 30%

profile of v2, /device:TPU:0, one launch (start us, length us, event | category | flops | bytes accessed | tf_op | source)
XLA Modules:
  0.0 78.8 jit_solution(4360496943488014094)
XLA Ops:
  1.0 1.6 %copy-done.1 = bf16[512,2048]{1,0:T(8,128)(2,1)S(1)} copy-done((bf16[512,2048]{1,0:T(8,128)(2,1)S(1)}, bf16[512,2048]{1,0:T(8,128)(2,1)}, u32[]{:S(2)}) %copy-start.1) | copy-done | bytes 2097176
  4.0 4.8 %project.1 = (bf16[512,512]{1,0:T(8,128)(2,1)S(1)}, bf16[512,512]{1,0:T(8,128)(2,1)S(1)}, bf16[512,2048]{1,0:T(8,128)(2,1)S(1)}, bf16[2048,512]{1,0:T(8,128)(2,1...) custom-call(bf16[512,2048]{1,0:T(8,128)(2,1)S(1)} %copy-done.1, ...), custom_call_target="tpu_custom_call" | custom-call | flops 2147483648 | tf_op jit(solution)/shard_map/project/pallas_call | solution.py:151
  8.8 2.6 %collective-permute-start = (bf16[272,128]{1,0:T(8,128)(2,1)S(1)}, bf16[272,128]{1,0:T(8,128)(2,1)S(1)}, u32[]{:S(2)}, u32[]{:S(2)}) collective-permute-start(bf16[272,128]{1,0:T(8,128)(2,1)S(1)} %get-tuple-element.27), channel_id=1, source_target_pairs={{0,4},{4,0},{8,12},{12,8},{16,20},{20,16},{24,28},{28,24},{1,5},{5... | collective-permute-start | bytes 208904 | tf_op jit(solution)/shard_map/ppermute | solution.py:80
  11.4 1.2 %queries.1.q = bf16[512,512]{1,0:T(8,128)(2,1)S(1)} custom-call(bf16[512,2048]{1,0:T(8,128)(2,1)S(1)} %get-tuple-element.23.normed, bf16[2048,512]{1,0:T(8,128)(2,1)S(1)} %get-tuple-element.24.weight), custom_call_target="tpu_custom_call" | custom-call | flops 1073741824 | tf_op jit(solution)/shard_map/queries/pallas_call | solution.py:174
  12.7 1.6 %collective-permute-done.got = bf16[272,128]{1,0:T(8,128)(2,1)S(1)} collective-permute-done((bf16[272,128]{1,0:T(8,128)(2,1)S(1)}, bf16[272,128]{1,0:T(8,128)(2,1)S(1)}, u32[]{:S(2)}, u32[]{:S(2)}) %collective-permute-start) | collective-permute-done | bytes 69664 | tf_op jit(solution)/shard_map/ppermute | solution.py:80
  14.3 1.9 %collective-permute-start.1 = (bf16[272,128]{1,0:T(8,128)(2,1)S(1)}, bf16[272,128]{1,0:T(8,128)(2,1)S(1)}, u32[]{:S(2)}, u32[]{:S(2)}) collective-permute-start(bf16[272,128]{1,0:T(8,128)(2,1)S(1)} %get-tuple-element.30), channel_id=1, source_target_pairs={{0,8},{4,12},{8,0},{12,4},{16,24},{20,28},{24,16},{28,20},{1,9},{5... | collective-permute-start | bytes 208904 | tf_op jit(solution)/shard_map/ppermute | solution.py:80
  16.2 1.5 %shard_map.83.refs_1_ = f32[512,256]{1,0:T(8,128)S(1)} custom-call(bf16[512,512]{1,0:T(8,128)(2,1)S(1)} %queries.1.q, bf16[512,512]{1,0:T(8,128)(2,1)S(1)} %get-tuple-element.34.k, bf16[512,512]{1,0:T(8,128)(2,1)S(1)} %get-tuple-element.35.v, f32[512,8]{1,0:T(8,128)S(1)} %get-tuple-element.25.column, f32[8,512]{1,0:T(8,128)S(1)} %get-tuple-element.36.row), custom_call_target="tpu_custom_call" | custom-call | flops 1073741824 | tf_op jit(solution)/shard_map/pallas_call | solution.py:217
  17.6 1.0 %collective-permute-done.1.got = bf16[272,128]{1,0:T(8,128)(2,1)S(1)} collective-permute-done((bf16[272,128]{1,0:T(8,128)(2,1)S(1)}, bf16[272,128]{1,0:T(8,128)(2,1)S(1)}, u32[]{:S(2)}, u32[]{:S(2)}) %collective-permute-start.1) | collective-permute-done | bytes 69664 | tf_op jit(solution)/shard_map/ppermute | solution.py:80
  18.7 2.9 %collective-permute-start.2 = (bf16[272,128]{1,0:T(8,128)(2,1)S(1)}, bf16[272,128]{1,0:T(8,128)(2,1)S(1)}, u32[]{:S(2)}, u32[]{:S(2)}) collective-permute-start(bf16[272,128]{1,0:T(8,128)(2,1)S(1)} %get-tuple-element.33), channel_id=1, source_target_pairs={{0,16},{4,20},{8,24},{12,28},{16,0},{20,4},{24,8},{28,12},{1,17},{... | collective-permute-start | bytes 208904 | tf_op jit(solution)/shard_map/ppermute | solution.py:80
  21.6 1.5 %shard_map.82.refs_0_ = f32[512,256]{1,0:T(8,128)S(1)} custom-call(bf16[512,512]{1,0:T(8,128)(2,1)S(1)} %queries.1.q, bf16[512,512]{1,0:T(8,128)(2,1)S(1)} %get-tuple-element.34.k, bf16[512,512]{1,0:T(8,128)(2,1)S(1)} %get-tuple-element.35.v, f32[512,8]{1,0:T(8,128)S(1)} %get-tuple-element.25.column, f32[8,512]{1,0:T(8,128)S(1)} %get-tuple-element.36.row), custom_call_target="tpu_custom_call" | custom-call | flops 1073741824 | tf_op jit(solution)/shard_map/pallas_call | solution.py:217
  26.8 1.8 %collective-permute-start.13 = (bf16[128,2048]{1,0:T(8,128)(2,1)S(1)}, bf16[128,2048]{1,0:T(8,128)(2,1)S(1)}, u32[]{:S(2)}, u32[]{:S(2)}) collective-permute-start(bf16[128,2048]{1,0:T(8,128)(2,1)S(1)} %project_heads.3.own), channel_id=1, source_target_pairs={{0,2},{1,3},{2,0},{3,1},{4,6},{5,7},{6,4},{7,5},{8,10},{9,11},{10,... | collective-permute-start | bytes 1572872 | tf_op jit(solution)/shard_map/ppermute | solution.py:75
  31.8 9.9 %collective-permute-done.13.refs_0_ = bf16[128,2048]{1,0:T(8,128)(2,1)S(1)} collective-permute-done((bf16[128,2048]{1,0:T(8,128)(2,1)S(1)}, bf16[128,2048]{1,0:T(8,128)(2,1)S(1)}, u32[]{:S(2)}, u32[]{:S(2)}) %collective-permute-start.13) | collective-permute-done | bytes 524320 | tf_op jit(solution)/shard_map/ppermute | solution.py:75
  42.2 2.7 %expand.3.hidden = bf16[128,2048]{1,0:T(8,128)(2,1)S(1)} custom-call(bf16[128,2048]{1,0:T(8,128)(2,1)S(1)} %get-tuple-element.40.rows_in, bf16[2,2048,1024]{2,1,0:T(8,128)(2,1)S(1)} %bitcast.4, bf16[2,2048,1024]{2,1,0:T(8,128)(2,1)S(1)} %collective-permute-done.6.other), custom_call_target="tpu_custom_call" | custom-call | flops 2147483648 | tf_op jit(solution)/shard_map/expand/pallas_call | solution.py:369
  44.9 1.3 %shard_map.88.own = bf16[128,2048]{1,0:T(8,128)(2,1)S(1)} custom-call(bf16[128,2048]{1,0:T(8,128)(2,1)S(1)} %expand.3.hidden, bf16[1024,2048]{1,0:T(8,128)(2,1)S(1)} %copy-done, bf16[1024,2048]{1,0:T(8,128)(2,1)S(1)} %collective-permute-done.7.other), custom_call_target="tpu_custom_call" | custom-call | flops 1073741824 | tf_op jit(solution)/shard_map/pallas_call | solution.py:388
  46.2 1.8 %collective-permute-start.14 = (bf16[128,2048]{1,0:T(8,128)(2,1)S(1)}, bf16[128,2048]{1,0:T(8,128)(2,1)S(1)}, u32[]{:S(2)}, u32[]{:S(2)}) collective-permute-start(bf16[128,2048]{1,0:T(8,128)(2,1)S(1)} %shard_map.88.own), channel_id=1, source_target_pairs={{0,2},{1,3},{2,0},{3,1},{4,6},{5,7},{6,4},{7,5},{8,10},{9,11},{10,... | collective-permute-start | bytes 1572872 | tf_op jit(solution)/shard_map/ppermute | solution.py:75
  48.0 5.0 %collective-permute-done.5.refs_0_ = bf16[128,2048]{1,0:T(8,128)(2,1)S(1)} collective-permute-done((bf16[128,2048]{1,0:T(8,128)(2,1)S(1)}, bf16[128,2048]{1,0:T(8,128)(2,1)S(1)}, u32[]{:S(2)}, u32[]{:S(2)}) %collective-permute-start.5) | collective-permute-done | bytes 524320 | tf_op jit(solution)/shard_map/ppermute | solution.py:75
  53.3 2.5 %expand.2.hidden = bf16[128,2048]{1,0:T(8,128)(2,1)S(1)} custom-call(bf16[128,2048]{1,0:T(8,128)(2,1)S(1)} %get-tuple-element.38.rows_in, bf16[2,2048,1024]{2,1,0:T(8,128)(2,1)S(1)} %bitcast.4, bf16[2,2048,1024]{2,1,0:T(8,128)(2,1)S(1)} %collective-permute-done.6.other), custom_call_target="tpu_custom_call" | custom-call | flops 2147483648 | tf_op jit(solution)/shard_map/expand/pallas_call | solution.py:369
  56.6 1.7 %collective-permute-start.16 = (bf16[128,1024]{1,0:T(8,128)(2,1)S(1)}, bf16[128,1024]{1,0:T(8,128)(2,1)S(1)}, u32[]{:S(2)}, u32[]{:S(2)}) collective-permute-start(bf16[128,1024]{1,0:T(8,128)(2,1)S(1)} %shard_map.89.own), channel_id=1, source_target_pairs={{0,2},{1,3},{2,0},{3,1},{4,6},{5,7},{6,4},{7,5},{8,10},{9,11},{10,... | collective-permute-start | bytes 786440 | tf_op jit(solution)/shard_map/ppermute | solution.py:75
  58.3 5.8 %collective-permute-done.14.refs_0_ = bf16[128,2048]{1,0:T(8,128)(2,1)S(1)} collective-permute-done((bf16[128,2048]{1,0:T(8,128)(2,1)S(1)}, bf16[128,2048]{1,0:T(8,128)(2,1)S(1)}, u32[]{:S(2)}, u32[]{:S(2)}) %collective-permute-start.14) | collective-permute-done | bytes 524320 | tf_op jit(solution)/shard_map/ppermute | solution.py:75
  64.9 1.8 %collective-permute-start.8 = (bf16[128,512]{1,0:T(8,128)(2,1)S(1)}, bf16[128,512]{1,0:T(8,128)(2,1)S(1)}, u32[]{:S(2)}, u32[]{:S(2)}) collective-permute-start(bf16[128,512]{1,0:T(8,128)(2,1)S(1)} %shard_map.85.own), channel_id=1, source_target_pairs={{0,2},{1,3},{2,0},{3,1},{4,6},{5,7},{6,4},{7,5},{8,10},{9,11},{10,... | collective-permute-start | bytes 393224 | tf_op jit(solution)/shard_map/ppermute | solution.py:75
  66.7 3.1 %collective-permute-done.16.refs_0_ = bf16[128,1024]{1,0:T(8,128)(2,1)S(1)} collective-permute-done((bf16[128,1024]{1,0:T(8,128)(2,1)S(1)}, bf16[128,1024]{1,0:T(8,128)(2,1)S(1)}, u32[]{:S(2)}, u32[]{:S(2)}) %collective-permute-start.16) | collective-permute-done | bytes 262176 | tf_op jit(solution)/shard_map/ppermute | solution.py:75
  70.4 1.8 %collective-permute-start.10 = (bf16[128,512]{1,0:T(8,128)(2,1)S(1)}, bf16[128,512]{1,0:T(8,128)(2,1)S(1)}, u32[]{:S(2)}, u32[]{:S(2)}) collective-permute-start(bf16[128,512]{1,0:T(8,128)(2,1)S(1)} %shard_map.86.own), channel_id=1, source_target_pairs={{0,2},{1,3},{2,0},{3,1},{4,6},{5,7},{6,4},{7,5},{8,10},{9,11},{10,... | collective-permute-start | bytes 393224 | tf_op jit(solution)/shard_map/ppermute | solution.py:75
  72.5 3.9 %collective-permute-done.10.refs_0_ = bf16[128,512]{1,0:T(8,128)(2,1)S(1)} collective-permute-done((bf16[128,512]{1,0:T(8,128)(2,1)S(1)}, bf16[128,512]{1,0:T(8,128)(2,1)S(1)}, u32[]{:S(2)}, u32[]{:S(2)}) %collective-permute-start.10) | collective-permute-done | bytes 131104 | tf_op jit(solution)/shard_map/ppermute | solution.py:75
  76.6 1.2 %place.2.refs_4_ = bf16[512,2048]{1,0:T(8,128)(2,1)} custom-call(bf16[128,2048]{1,0:T(8,128)(2,1)S(1)} %add_partials.6.refs_0_, bf16[128,2048]{1,0:T(8,128)(2,1)S(1)} %collective-permute-done.15.refs_1_, bf16[128,1024]{1,0:T(8,128)(2,1)S(1)} %add_partials.7.refs_2_, bf16[128,1024]{1,0:T(8,128)(2,1)S(1)} %collective-permute-done.17.refs_3_), custom_call_target="tpu_custom_call" | custom-call | flops 268435456 | tf_op jit(solution)/shard_map/place/pallas_call | solution.py:437
  (56 shorter events, 13.6 us)
Async XLA Ops:
  0.0 42.1 %collective-permute-start.6 = (bf16[2,2048,1024]{2,1,0:T(8,128)(2,1)}, bf16[2,2048,1024]{2,1,0:T(8,128)(2,1)S(1)}, u32[]{:S(2)}, u32[]{:S(2)}) collective-permute-start(bf16[2,2048,1024]{2,1,0:T(8,128)(2,1)} %own.13), channel_id=1, source_target_pairs={{0,1},{1,0},{2,3},{3,2},{4,5},{5,4},{6,7},{7,6},{8,9},{9,8},{10,11... | collective-permute-start | bytes 25165832 | tf_op jit(solution)/shard_map/ppermute | solution.py:70
  0.5 44.4 %collective-permute-start.7 = (bf16[1024,2048]{1,0:T(8,128)(2,1)}, bf16[1024,2048]{1,0:T(8,128)(2,1)S(1)}, u32[]{:S(2)}, u32[]{:S(2)}) collective-permute-start(bf16[1024,2048]{1,0:T(8,128)(2,1)} %own.15), channel_id=1, source_target_pairs={{0,1},{1,0},{2,3},{3,2},{4,5},{5,4},{6,7},{7,6},{8,9},{9,8},{10,11... | collective-permute-start | bytes 12582920 | tf_op jit(solution)/shard_map/ppermute | solution.py:70
  0.5 25.5 %collective-permute-start.4 = (bf16[512,2048]{1,0:T(8,128)(2,1)}, bf16[512,2048]{1,0:T(8,128)(2,1)S(1)}, u32[]{:S(2)}, u32[]{:S(2)}) collective-permute-start(bf16[512,2048]{1,0:T(8,128)(2,1)} %own.12), channel_id=1, source_target_pairs={{0,1},{1,0},{2,3},{3,2},{4,5},{5,4},{6,7},{7,6},{8,9},{9,8},{10,11... | collective-permute-start | bytes 6291464 | tf_op jit(solution)/shard_map/ppermute | solution.py:70
  1.0 1.6 %copy-start.1 = (bf16[512,2048]{1,0:T(8,128)(2,1)S(1)}, bf16[512,2048]{1,0:T(8,128)(2,1)}, u32[]{:S(2)}) copy-start(bf16[512,2048]{1,0:T(8,128)(2,1)} %tok.5) | copy-start | bytes 6291460
  8.8 5.4 %collective-permute-start = (bf16[272,128]{1,0:T(8,128)(2,1)S(1)}, bf16[272,128]{1,0:T(8,128)(2,1)S(1)}, u32[]{:S(2)}, u32[]{:S(2)}) collective-permute-start(bf16[272,128]{1,0:T(8,128)(2,1)S(1)} %get-tuple-element.27), channel_id=1, source_target_pairs={{0,4},{4,0},{8,12},{12,8},{16,20},{20,16},{24,28},{28,24},{1,5},{5... | collective-permute-start | bytes 208904 | tf_op jit(solution)/shard_map/ppermute | solution.py:80
  14.3 4.4 %collective-permute-start.1 = (bf16[272,128]{1,0:T(8,128)(2,1)S(1)}, bf16[272,128]{1,0:T(8,128)(2,1)S(1)}, u32[]{:S(2)}, u32[]{:S(2)}) collective-permute-start(bf16[272,128]{1,0:T(8,128)(2,1)S(1)} %get-tuple-element.30), channel_id=1, source_target_pairs={{0,8},{4,12},{8,0},{12,4},{16,24},{20,28},{24,16},{28,20},{1,9},{5... | collective-permute-start | bytes 208904 | tf_op jit(solution)/shard_map/ppermute | solution.py:80
  18.7 5.3 %collective-permute-start.2 = (bf16[272,128]{1,0:T(8,128)(2,1)S(1)}, bf16[272,128]{1,0:T(8,128)(2,1)S(1)}, u32[]{:S(2)}, u32[]{:S(2)}) collective-permute-start(bf16[272,128]{1,0:T(8,128)(2,1)S(1)} %get-tuple-element.33), channel_id=1, source_target_pairs={{0,16},{4,20},{8,24},{12,28},{16,0},{20,4},{24,8},{28,12},{1,17},{... | collective-permute-start | bytes 208904 | tf_op jit(solution)/shard_map/ppermute | solution.py:80
  24.0 2.0 %copy-start.2 = (bf16[512,2048]{1,0:T(8,128)(2,1)S(1)}, bf16[512,2048]{1,0:T(8,128)(2,1)}, u32[]{:S(2)}) copy-start(bf16[512,2048]{1,0:T(8,128)(2,1)} %own.12) | copy-start | bytes 6291460
  24.6 1.4 %collective-permute-start.12 = (bf16[128,512]{1,0:T(8,128)(2,1)S(1)}, bf16[128,512]{1,0:T(8,128)(2,1)S(1)}, u32[]{:S(2)}, u32[]{:S(2)}) collective-permute-start(bf16[128,512]{1,0:T(8,128)(2,1)S(1)} %finish_heads.7), channel_id=1, source_target_pairs={{0,1},{1,0},{2,3},{3,2},{4,5},{5,4},{6,7},{7,6},{8,9},{9,8},{10,11... | collective-permute-start | bytes 393224 | tf_op jit(solution)/shard_map/ppermute | solution.py:70
  26.1 16.1 %slice-start = ((s8[8388608]{0:T(1024)(128)(4,1)}), s8[4194304]{0:T(1024)(128)(4,1)S(1)}, s32[]{:S(2)}) async-start(s8[8388608]{0:T(1024)(128)(4,1)} %bitcast.3), calls=%async_computation | async-start | bytes 8388608
  26.8 14.9 %collective-permute-start.13 = (bf16[128,2048]{1,0:T(8,128)(2,1)S(1)}, bf16[128,2048]{1,0:T(8,128)(2,1)S(1)}, u32[]{:S(2)}, u32[]{:S(2)}) collective-permute-start(bf16[128,2048]{1,0:T(8,128)(2,1)S(1)} %project_heads.3.own), channel_id=1, source_target_pairs={{0,2},{1,3},{2,0},{3,1},{4,6},{5,7},{6,4},{7,5},{8,10},{9,11},{10,... | collective-permute-start | bytes 1572872 | tf_op jit(solution)/shard_map/ppermute | solution.py:75
  29.2 12.9 %slice-start.1 = ((s8[8388608]{0:T(1024)(128)(4,1)}), s8[4194304]{0:T(1024)(128)(4,1)S(1)}, s32[]{:S(2)}) async-start(s8[8388608]{0:T(1024)(128)(4,1)} %bitcast.3), calls=%async_computation.1 | async-start | bytes 8388608
  29.2 1.4 %collective-permute-start.3 = (bf16[128,512]{1,0:T(8,128)(2,1)S(1)}, bf16[128,512]{1,0:T(8,128)(2,1)S(1)}, u32[]{:S(2)}, u32[]{:S(2)}) collective-permute-start(bf16[128,512]{1,0:T(8,128)(2,1)S(1)} %finish_heads.5), channel_id=1, source_target_pairs={{0,1},{1,0},{2,3},{3,2},{4,5},{5,4},{6,7},{7,6},{8,9},{9,8},{10,11... | collective-permute-start | bytes 393224 | tf_op jit(solution)/shard_map/ppermute | solution.py:70
  29.9 11.8 %copy-start.3 = (f32[2048]{0:T(1024)S(1)}, f32[2048]{0:T(1024)}, u32[]{:S(2)}) copy-start(f32[2048]{0:T(1024)} %param.13) | copy-start | bytes 24580
  31.4 21.6 %collective-permute-start.5 = (bf16[128,2048]{1,0:T(8,128)(2,1)S(1)}, bf16[128,2048]{1,0:T(8,128)(2,1)S(1)}, u32[]{:S(2)}, u32[]{:S(2)}) collective-permute-start(bf16[128,2048]{1,0:T(8,128)(2,1)S(1)} %project_heads.2.own), channel_id=1, source_target_pairs={{0,2},{1,3},{2,0},{3,1},{4,6},{5,7},{6,4},{7,5},{8,10},{9,11},{10,... | collective-permute-start | bytes 1572872 | tf_op jit(solution)/shard_map/ppermute | solution.py:75
  42.1 2.8 %copy-start = (bf16[1024,2048]{1,0:T(8,128)(2,1)S(1)}, bf16[1024,2048]{1,0:T(8,128)(2,1)}, u32[]{:S(2)}) copy-start(bf16[1024,2048]{1,0:T(8,128)(2,1)} %own.15) | copy-start | bytes 12582916
  46.2 18.0 %collective-permute-start.14 = (bf16[128,2048]{1,0:T(8,128)(2,1)S(1)}, bf16[128,2048]{1,0:T(8,128)(2,1)S(1)}, u32[]{:S(2)}, u32[]{:S(2)}) collective-permute-start(bf16[128,2048]{1,0:T(8,128)(2,1)S(1)} %shard_map.88.own), channel_id=1, source_target_pairs={{0,2},{1,3},{2,0},{3,1},{4,6},{5,7},{6,4},{7,5},{8,10},{9,11},{10,... | collective-permute-start | bytes 1572872 | tf_op jit(solution)/shard_map/ppermute | solution.py:75
  56.6 13.2 %collective-permute-start.16 = (bf16[128,1024]{1,0:T(8,128)(2,1)S(1)}, bf16[128,1024]{1,0:T(8,128)(2,1)S(1)}, u32[]{:S(2)}, u32[]{:S(2)}) collective-permute-start(bf16[128,1024]{1,0:T(8,128)(2,1)S(1)} %shard_map.89.own), channel_id=1, source_target_pairs={{0,2},{1,3},{2,0},{3,1},{4,6},{5,7},{6,4},{7,5},{8,10},{9,11},{10,... | collective-permute-start | bytes 786440 | tf_op jit(solution)/shard_map/ppermute | solution.py:75
  64.4 12.2 %collective-permute-start.15 = (bf16[128,2048]{1,0:T(8,128)(2,1)S(1)}, bf16[128,2048]{1,0:T(8,128)(2,1)S(1)}, u32[]{:S(2)}, u32[]{:S(2)}) collective-permute-start(bf16[128,2048]{1,0:T(8,128)(2,1)S(1)} %add_partials.6.refs_0_), channel_id=1, source_target_pairs={{0,1},{1,0},{2,3},{3,2},{4,5},{5,4},{6,7},{7,6},{8,9},{9,8},{10,11... | collective-permute-start | bytes 1572872 | tf_op jit(solution)/shard_map/ppermute | solution.py:70
  64.9 7.3 %collective-permute-start.8 = (bf16[128,512]{1,0:T(8,128)(2,1)S(1)}, bf16[128,512]{1,0:T(8,128)(2,1)S(1)}, u32[]{:S(2)}, u32[]{:S(2)}) collective-permute-start(bf16[128,512]{1,0:T(8,128)(2,1)S(1)} %shard_map.85.own), channel_id=1, source_target_pairs={{0,2},{1,3},{2,0},{3,1},{4,6},{5,7},{6,4},{7,5},{8,10},{9,11},{10,... | collective-permute-start | bytes 393224 | tf_op jit(solution)/shard_map/ppermute | solution.py:75
  69.9 6.6 %collective-permute-start.17 = (bf16[128,1024]{1,0:T(8,128)(2,1)S(1)}, bf16[128,1024]{1,0:T(8,128)(2,1)S(1)}, u32[]{:S(2)}, u32[]{:S(2)}) collective-permute-start(bf16[128,1024]{1,0:T(8,128)(2,1)S(1)} %add_partials.7.refs_2_), channel_id=1, source_target_pairs={{0,1},{1,0},{2,3},{3,2},{4,5},{5,4},{6,7},{7,6},{8,9},{9,8},{10,11... | collective-permute-start | bytes 786440 | tf_op jit(solution)/shard_map/ppermute | solution.py:70
  70.4 6.0 %collective-permute-start.10 = (bf16[128,512]{1,0:T(8,128)(2,1)S(1)}, bf16[128,512]{1,0:T(8,128)(2,1)S(1)}, u32[]{:S(2)}, u32[]{:S(2)}) collective-permute-start(bf16[128,512]{1,0:T(8,128)(2,1)S(1)} %shard_map.86.own), channel_id=1, source_target_pairs={{0,2},{1,3},{2,0},{3,1},{4,6},{5,7},{6,4},{7,5},{8,10},{9,11},{10,... | collective-permute-start | bytes 393224 | tf_op jit(solution)/shard_map/ppermute | solution.py:75
  72.3 5.5 %collective-permute-start.9 = (bf16[128,512]{1,0:T(8,128)(2,1)S(1)}, bf16[128,512]{1,0:T(8,128)(2,1)S(1)}, u32[]{:S(2)}, u32[]{:S(2)}) collective-permute-start(bf16[128,512]{1,0:T(8,128)(2,1)S(1)} %add_partials.4.refs_0_), channel_id=1, source_target_pairs={{0,1},{1,0},{2,3},{3,2},{4,5},{5,4},{6,7},{7,6},{8,9},{9,8},{10,11... | collective-permute-start | bytes 393224 | tf_op jit(solution)/shard_map/ppermute | solution.py:70
  76.5 1.4 %collective-permute-start.11 = (bf16[128,512]{1,0:T(8,128)(2,1)S(1)}, bf16[128,512]{1,0:T(8,128)(2,1)S(1)}, u32[]{:S(2)}, u32[]{:S(2)}) collective-permute-start(bf16[128,512]{1,0:T(8,128)(2,1)S(1)} %add_partials.5.refs_2_), channel_id=1, source_target_pairs={{0,1},{1,0},{2,3},{3,2},{4,5},{5,4},{6,7},{7,6},{8,9},{9,8},{10,11... | collective-permute-start | bytes 393224 | tf_op jit(solution)/shard_map/ppermute | solution.py:70
  (2 other events, 1.4 us)

commit v3 on v2

--- a/solution.py
+++ b/solution.py
@@ -81,18 +81,14 @@
 
 
 def project_kernel(
-    size, tok, gain, forget, weight, keys, values, normed, query_weight, column, row, state, sent, tok_here, weight_here, sems
+    size, opened, tok, gain, forget, weight, keys, values, normed, query_weight, column, row, state, sent, weight_here, sems
 ):
     heads, rows = forget.shape
-    parts = 4
-    span = rows // parts
+    targets = (weight_here.at[0], weight_here.at[1], query_weight)
     loads = [
-        pltpu.make_async_copy(tok.at[pl.ds(p * span, span)], tok_here.at[pl.ds(p * span, span)], sems.at[p])
-        for p in range(parts)
+        pltpu.make_async_copy(weight.at[which], target, sems.at[at])
+        for at, (which, target) in enumerate(zip((1, 2, 0), targets))
     ]
-    for which in (1, 2):
-        loads.append(pltpu.make_async_copy(weight.at[which], weight_here.at[which - 1], sems.at[parts + which - 1]))
-    loads.append(pltpu.make_async_copy(weight.at[0], query_weight, sems.at[parts + 2]))
     for load in loads:
         load.start()
 
@@ -106,13 +102,10 @@
     ends = grown[rows - 1 :, :]
     decays = jnp.exp2(ends)
 
-    for p in range(parts):
-        loads[p].wait()
-        here = pl.ds(p * span, span)
-        normed[here, :] = normalize(tok_here[here, :].astype(f32), gain[...])
-    loads[parts].wait()
+    normed[...] = normalize(tok[...].astype(f32), gain[...])
+    loads[0].wait()
     keys[...] = dot(normed[...], weight_here[0]).astype(bf16)
-    loads[parts + 1].wait()
+    loads[1].wait()
     values[...] = dot(normed[...], weight_here[1]).astype(bf16)
 
     lanes = 2 * size
@@ -130,10 +123,25 @@
     base = heads // 2 * size
     state[pl.ds(base, 16), :] = picked
     sent[pl.ds(base, 16), :] = picked.astype(bf16)
-    loads[parts + 2].wait()
-
-
-def project(tokens, gain, forget, projections, size):
+    loads[2].wait()
+
+
+def open_kernel(out):
+    out[...] = jnp.zeros_like(out)
+
+
+def opening():
+    return pl.pallas_call(
+        open_kernel,
+        out_specs=vmem,
+        out_shape=jax.ShapeDtypeStruct((8, 128), f32),
+        compiler_params=room(1),
+        cost_estimate=cost(1 << 32),
+        name="opening",
+    )()
+
+
+def project(opened, tokens, gain, forget, projections, size):
     rows, width = tokens.shape
     heads = forget.shape[1]
     mine = projections.shape[2]
@@ -150,18 +158,17 @@
     ]
     return pl.pallas_call(
         functools.partial(project_kernel, size),
-        in_specs=[hbm, vmem, vmem, hbm],
+        in_specs=[hbm, vmem, vmem, vmem, hbm],
         out_specs=[vmem] * len(outs),
         out_shape=[jax.ShapeDtypeStruct(shape, kind) for shape, kind in outs],
         scratch_shapes=[
-            pltpu.VMEM((rows, width), bf16),
             pltpu.VMEM((2, width, mine), bf16),
-            pltpu.SemaphoreType.DMA((7,)),
+            pltpu.SemaphoreType.DMA((3,)),
         ],
         cost_estimate=cost(4 * rows * width * mine),
         compiler_params=room(42),
         name="project",
-    )(tokens, gain.reshape(1, width), forget.T, projections)
+    )(opened, tokens, gain.reshape(1, width), forget.T, projections)
 
 
 def query_kernel(scale, normed, weight, out):
@@ -459,7 +466,7 @@
     down_other = swap_cores(down_weight)
 
     k, v, normed, query_weight, column, row, state, sent = project(
-        tokens, attn_gain, forget, projections, head_size
+        opening(), tokens, attn_gain, forget, projections, head_size
     )
     before = incoming_state(state, sent, head_size)
     q = queries(normed, query_weight, head_size)

time: 79.2 us -> 76.7 us (0.968)
  starting transfers between devices: 18.1 us -> 20.7 us
  local copies, waits for them, and re-layouts: 3.03 us -> 0.55 us
  waiting for transfers between devices: 32.9 us -> 31 us
    unnamed x16, local copies, waits for them, and re-layouts: 3.03 us -> 0.55 us
    ppermute x6, starting transfers between devices: 9.15 us -> 10.7 us  [across_chips(): lax.ppermute(value, 'tp', [(i, (i + cores) % count) for i in range(count)])]
    ppermute x3, starting transfers between devices: 7.31 us -> 8.3 us  [with_seq(): return lax.ppermute(value, 'seq', [(i, i ^ bit) for i in range(count)])]
    ppermute x6, waiting for transfers between devices: 27.7 us -> 26.8 us  [across_chips(): lax.ppermute(value, 'tp', [(i, (i + cores) % count) for i in range(count)])]
    ppermute x3, waiting for transfers between devices: 3.56 us -> 2.66 us  [with_seq(): return lax.ppermute(value, 'seq', [(i, i ^ bit) for i in range(count)])]
where the time goes in v3:
time: 76.7 us; the launch traced here: 76.6 us
  waiting for transfers between devices  31 us (40%)
  Pallas kernels  23.8 us (31%)
  starting transfers between devices  20.7 us (27%)
    ppermute x6, waiting for transfers between devices, across_chips(): lax.ppermute(value, 'tp', [(i, (i + cores) % count) for i in range(count)])  26.8 us
    ppermute x6, starting transfers between devices, across_chips(): lax.ppermute(value, 'tp', [(i, (i + cores) % count) for i in range(count)])  10.7 us
    ppermute x3, starting transfers between devices, with_seq(): return lax.ppermute(value, 'seq', [(i, i ^ bit) for i in range(count)])  8.3 us
    pallas_call x2, Pallas kernels, expand(): pl.pallas_call(expand_kernel, in_specs=[vmem] * 3, out_specs=vmem, out_sh...  5.17 us
    pallas_call x1, Pallas kernels, project(): pl.pallas_call(functools.partial(project_kernel, size), in_specs=[hbm, vm...  4.46 us
    pallas_call x2, Pallas kernels, block_attention(): pl.pallas_call(functools.partial(block_kernel, size, first_pair, heads //...  2.95 us
    pallas_call x4, Pallas kernels, down(): pl.pallas_call(functools.partial(down_kernel, start), in_specs=[vmem] * 3...  2.92 us
    ppermute x3, waiting for transfers between devices, with_seq(): return lax.ppermute(value, 'seq', [(i, i ^ bit) for i in range(count)])  2.66 us
  transfers between devices with their start and end apart: 18, of which 11 were waited for; matrix products, arithmetic and copies ran while one was open for 0% of the time, Pallas kernels for 30%

profile of v3, /device:TPU:0, one launch (start us, length us, event | category | flops | bytes accessed | tf_op | source)
XLA Modules:
  0.0 76.6 jit_solution(4077955266962647931)
XLA Ops:
  1.6 4.5 %project.1 = (bf16[512,512]{1,0:T(8,128)(2,1)S(1)}, bf16[512,512]{1,0:T(8,128)(2,1)S(1)}, bf16[512,2048]{1,0:T(8,128)(2,1)S(1)}, bf16[2048,512]{1,0:T(8,128)(2,1...) custom-call(f32[8,128]{1,0:T(8,128)S(1)} %opening.1.opened, ...), custom_call_target="tpu_custom_call" | custom-call | flops 2147483648 | tf_op jit(solution)/shard_map/project/pallas_call | solution.py:159
  6.1 3.1 %collective-permute-start = (bf16[272,128]{1,0:T(8,128)(2,1)S(1)}, bf16[272,128]{1,0:T(8,128)(2,1)S(1)}, u32[]{:S(2)}, u32[]{:S(2)}) collective-permute-start(bf16[272,128]{1,0:T(8,128)(2,1)S(1)} %get-tuple-element.27), channel_id=1, source_target_pairs={{0,4},{4,0},{8,12},{12,8},{16,20},{20,16},{24,28},{28,24},{1,5},{5... | collective-permute-start | bytes 208904 | tf_op jit(solution)/shard_map/ppermute | solution.py:80
  9.1 1.2 %queries.1.q = bf16[512,512]{1,0:T(8,128)(2,1)S(1)} custom-call(bf16[512,2048]{1,0:T(8,128)(2,1)S(1)} %get-tuple-element.23.normed, bf16[2048,512]{1,0:T(8,128)(2,1)S(1)} %get-tuple-element.24.weight), custom_call_target="tpu_custom_call" | custom-call | flops 1073741824 | tf_op jit(solution)/shard_map/queries/pallas_call | solution.py:181
  10.4 1.0 %collective-permute-done.got = bf16[272,128]{1,0:T(8,128)(2,1)S(1)} collective-permute-done((bf16[272,128]{1,0:T(8,128)(2,1)S(1)}, bf16[272,128]{1,0:T(8,128)(2,1)S(1)}, u32[]{:S(2)}, u32[]{:S(2)}) %collective-permute-start) | collective-permute-done | bytes 69664 | tf_op jit(solution)/shard_map/ppermute | solution.py:80
  11.5 2.1 %collective-permute-start.1 = (bf16[272,128]{1,0:T(8,128)(2,1)S(1)}, bf16[272,128]{1,0:T(8,128)(2,1)S(1)}, u32[]{:S(2)}, u32[]{:S(2)}) collective-permute-start(bf16[272,128]{1,0:T(8,128)(2,1)S(1)} %get-tuple-element.30), channel_id=1, source_target_pairs={{0,8},{4,12},{8,0},{12,4},{16,24},{20,28},{24,16},{28,20},{1,9},{5... | collective-permute-start | bytes 208904 | tf_op jit(solution)/shard_map/ppermute | solution.py:80
  13.6 1.5 %shard_map.83.refs_1_ = f32[512,256]{1,0:T(8,128)S(1)} custom-call(bf16[512,512]{1,0:T(8,128)(2,1)S(1)} %queries.1.q, bf16[512,512]{1,0:T(8,128)(2,1)S(1)} %get-tuple-element.34.k, bf16[512,512]{1,0:T(8,128)(2,1)S(1)} %get-tuple-element.35.v, f32[512,8]{1,0:T(8,128)S(1)} %get-tuple-element.25.column, f32[8,512]{1,0:T(8,128)S(1)} %get-tuple-element.36.row), custom_call_target="tpu_custom_call" | custom-call | flops 1073741824 | tf_op jit(solution)/shard_map/pallas_call | solution.py:224
  15.9 3.1 %collective-permute-start.2 = (bf16[272,128]{1,0:T(8,128)(2,1)S(1)}, bf16[272,128]{1,0:T(8,128)(2,1)S(1)}, u32[]{:S(2)}, u32[]{:S(2)}) collective-permute-start(bf16[272,128]{1,0:T(8,128)(2,1)S(1)} %get-tuple-element.33), channel_id=1, source_target_pairs={{0,16},{4,20},{8,24},{12,28},{16,0},{20,4},{24,8},{28,12},{1,17},{... | collective-permute-start | bytes 208904 | tf_op jit(solution)/shard_map/ppermute | solution.py:80
  19.0 1.5 %shard_map.82.refs_0_ = f32[512,256]{1,0:T(8,128)S(1)} custom-call(bf16[512,512]{1,0:T(8,128)(2,1)S(1)} %queries.1.q, bf16[512,512]{1,0:T(8,128)(2,1)S(1)} %get-tuple-element.34.k, bf16[512,512]{1,0:T(8,128)(2,1)S(1)} %get-tuple-element.35.v, f32[512,8]{1,0:T(8,128)S(1)} %get-tuple-element.25.column, f32[8,512]{1,0:T(8,128)S(1)} %get-tuple-element.36.row), custom_call_target="tpu_custom_call" | custom-call | flops 1073741824 | tf_op jit(solution)/shard_map/pallas_call | solution.py:224
  20.5 0.8 %collective-permute-done.2.got = bf16[272,128]{1,0:T(8,128)(2,1)S(1)} collective-permute-done((bf16[272,128]{1,0:T(8,128)(2,1)S(1)}, bf16[272,128]{1,0:T(8,128)(2,1)S(1)}, u32[]{:S(2)}, u32[]{:S(2)}) %collective-permute-start.2) | collective-permute-done | bytes 69664 | tf_op jit(solution)/shard_map/ppermute | solution.py:80
  24.1 2.3 %collective-permute-start.13 = (bf16[128,2048]{1,0:T(8,128)(2,1)S(1)}, bf16[128,2048]{1,0:T(8,128)(2,1)S(1)}, u32[]{:S(2)}, u32[]{:S(2)}) collective-permute-start(bf16[128,2048]{1,0:T(8,128)(2,1)S(1)} %project_heads.3.own), channel_id=1, source_target_pairs={{0,2},{1,3},{2,0},{3,1},{4,6},{5,7},{6,4},{7,5},{8,10},{9,11},{10,... | collective-permute-start | bytes 1572872 | tf_op jit(solution)/shard_map/ppermute | solution.py:75
  29.2 9.9 %collective-permute-done.13.refs_0_ = bf16[128,2048]{1,0:T(8,128)(2,1)S(1)} collective-permute-done((bf16[128,2048]{1,0:T(8,128)(2,1)S(1)}, bf16[128,2048]{1,0:T(8,128)(2,1)S(1)}, u32[]{:S(2)}, u32[]{:S(2)}) %collective-permute-start.13) | collective-permute-done | bytes 524320 | tf_op jit(solution)/shard_map/ppermute | solution.py:75
  39.6 2.7 %expand.3.hidden = bf16[128,2048]{1,0:T(8,128)(2,1)S(1)} custom-call(bf16[128,2048]{1,0:T(8,128)(2,1)S(1)} %get-tuple-element.40.rows_in, bf16[2,2048,1024]{2,1,0:T(8,128)(2,1)S(1)} %bitcast.4, bf16[2,2048,1024]{2,1,0:T(8,128)(2,1)S(1)} %collective-permute-done.6.other), custom_call_target="tpu_custom_call" | custom-call | flops 2147483648 | tf_op jit(solution)/shard_map/expand/pallas_call | solution.py:376
  42.4 1.3 %shard_map.88.own = bf16[128,2048]{1,0:T(8,128)(2,1)S(1)} custom-call(bf16[128,2048]{1,0:T(8,128)(2,1)S(1)} %expand.3.hidden, bf16[1024,2048]{1,0:T(8,128)(2,1)S(1)} %copy-done, bf16[1024,2048]{1,0:T(8,128)(2,1)S(1)} %collective-permute-done.7.other), custom_call_target="tpu_custom_call" | custom-call | flops 1073741824 | tf_op jit(solution)/shard_map/pallas_call | solution.py:395
  43.6 2.1 %collective-permute-start.14 = (bf16[128,2048]{1,0:T(8,128)(2,1)S(1)}, bf16[128,2048]{1,0:T(8,128)(2,1)S(1)}, u32[]{:S(2)}, u32[]{:S(2)}) collective-permute-start(bf16[128,2048]{1,0:T(8,128)(2,1)S(1)} %shard_map.88.own), channel_id=1, source_target_pairs={{0,2},{1,3},{2,0},{3,1},{4,6},{5,7},{6,4},{7,5},{8,10},{9,11},{10,... | collective-permute-start | bytes 1572872 | tf_op jit(solution)/shard_map/ppermute | solution.py:75
  45.7 4.7 %collective-permute-done.5.refs_0_ = bf16[128,2048]{1,0:T(8,128)(2,1)S(1)} collective-permute-done((bf16[128,2048]{1,0:T(8,128)(2,1)S(1)}, bf16[128,2048]{1,0:T(8,128)(2,1)S(1)}, u32[]{:S(2)}, u32[]{:S(2)}) %collective-permute-start.5) | collective-permute-done | bytes 524320 | tf_op jit(solution)/shard_map/ppermute | solution.py:75
  50.8 2.5 %expand.2.hidden = bf16[128,2048]{1,0:T(8,128)(2,1)S(1)} custom-call(bf16[128,2048]{1,0:T(8,128)(2,1)S(1)} %get-tuple-element.38.rows_in, bf16[2,2048,1024]{2,1,0:T(8,128)(2,1)S(1)} %bitcast.4, bf16[2,2048,1024]{2,1,0:T(8,128)(2,1)S(1)} %collective-permute-done.6.other), custom_call_target="tpu_custom_call" | custom-call | flops 2147483648 | tf_op jit(solution)/shard_map/expand/pallas_call | solution.py:376
  54.0 2.1 %collective-permute-start.16 = (bf16[128,1024]{1,0:T(8,128)(2,1)S(1)}, bf16[128,1024]{1,0:T(8,128)(2,1)S(1)}, u32[]{:S(2)}, u32[]{:S(2)}) collective-permute-start(bf16[128,1024]{1,0:T(8,128)(2,1)S(1)} %shard_map.89.own), channel_id=1, source_target_pairs={{0,2},{1,3},{2,0},{3,1},{4,6},{5,7},{6,4},{7,5},{8,10},{9,11},{10,... | collective-permute-start | bytes 786440 | tf_op jit(solution)/shard_map/ppermute | solution.py:75
  56.1 5.5 %collective-permute-done.14.refs_0_ = bf16[128,2048]{1,0:T(8,128)(2,1)S(1)} collective-permute-done((bf16[128,2048]{1,0:T(8,128)(2,1)S(1)}, bf16[128,2048]{1,0:T(8,128)(2,1)S(1)}, u32[]{:S(2)}, u32[]{:S(2)}) %collective-permute-start.14) | collective-permute-done | bytes 524320 | tf_op jit(solution)/shard_map/ppermute | solution.py:75
  62.4 2.1 %collective-permute-start.8 = (bf16[128,512]{1,0:T(8,128)(2,1)S(1)}, bf16[128,512]{1,0:T(8,128)(2,1)S(1)}, u32[]{:S(2)}, u32[]{:S(2)}) collective-permute-start(bf16[128,512]{1,0:T(8,128)(2,1)S(1)} %shard_map.85.own), channel_id=1, source_target_pairs={{0,2},{1,3},{2,0},{3,1},{4,6},{5,7},{6,4},{7,5},{8,10},{9,11},{10,... | collective-permute-start | bytes 393224 | tf_op jit(solution)/shard_map/ppermute | solution.py:75
  64.5 2.8 %collective-permute-done.16.refs_0_ = bf16[128,1024]{1,0:T(8,128)(2,1)S(1)} collective-permute-done((bf16[128,1024]{1,0:T(8,128)(2,1)S(1)}, bf16[128,1024]{1,0:T(8,128)(2,1)S(1)}, u32[]{:S(2)}, u32[]{:S(2)}) %collective-permute-start.16) | collective-permute-done | bytes 262176 | tf_op jit(solution)/shard_map/ppermute | solution.py:75
  67.9 2.1 %collective-permute-start.10 = (bf16[128,512]{1,0:T(8,128)(2,1)S(1)}, bf16[128,512]{1,0:T(8,128)(2,1)S(1)}, u32[]{:S(2)}, u32[]{:S(2)}) collective-permute-start(bf16[128,512]{1,0:T(8,128)(2,1)S(1)} %shard_map.86.own), channel_id=1, source_target_pairs={{0,2},{1,3},{2,0},{3,1},{4,6},{5,7},{6,4},{7,5},{8,10},{9,11},{10,... | collective-permute-start | bytes 393224 | tf_op jit(solution)/shard_map/ppermute | solution.py:75
  70.3 3.8 %collective-permute-done.10.refs_0_ = bf16[128,512]{1,0:T(8,128)(2,1)S(1)} collective-permute-done((bf16[128,512]{1,0:T(8,128)(2,1)S(1)}, bf16[128,512]{1,0:T(8,128)(2,1)S(1)}, u32[]{:S(2)}, u32[]{:S(2)}) %collective-permute-start.10) | collective-permute-done | bytes 131104 | tf_op jit(solution)/shard_map/ppermute | solution.py:75
  74.3 1.2 %place.2.refs_4_ = bf16[512,2048]{1,0:T(8,128)(2,1)} custom-call(bf16[128,2048]{1,0:T(8,128)(2,1)S(1)} %add_partials.6.refs_0_, bf16[128,2048]{1,0:T(8,128)(2,1)S(1)} %collective-permute-done.15.refs_1_, bf16[128,1024]{1,0:T(8,128)(2,1)S(1)} %add_partials.7.refs_2_, bf16[128,1024]{1,0:T(8,128)(2,1)S(1)} %collective-permute-done.17.refs_3_), custom_call_target="tpu_custom_call" | custom-call | flops 268435456 | tf_op jit(solution)/shard_map/place/pallas_call | solution.py:444
  75.6 0.8 %place.3 = bf16[512,2048]{1,0:T(8,128)(2,1)} custom-call(bf16[128,512]{1,0:T(8,128)(2,1)S(1)} %add_partials.4.refs_0_, bf16[128,512]{1,0:T(8,128)(2,1)S(1)} %collective-permute-done.9.refs_1_, bf16[128,512]{1,0:T(8,128)(2,1)S(1)} %add_partials.5.refs_2_, bf16[128,512]{1,0:T(8,128)(2,1)S(1)} %collective-permute-done.11.refs_3_, ...), custom_call_target="tpu_custom_call", output_to_operand_aliasing={{}: (4, {})} | custom-call | flops 268435456 | tf_op jit(solution)/shard_map/place/pallas_call | solution.py:444
  (57 shorter events, 11.5 us)
Async XLA Ops:
  0.0 1.6 %copy-start.4 = (f32[512,8]{0,1:T(8,128)S(1)}, f32[512,8]{0,1:T(8,128)}, u32[]{:S(2)}) copy-start(f32[512,8]{0,1:T(8,128)} %param.9) | copy-start | bytes 49156
  0.0 39.6 %collective-permute-start.6 = (bf16[2,2048,1024]{2,1,0:T(8,128)(2,1)}, bf16[2,2048,1024]{2,1,0:T(8,128)(2,1)S(1)}, u32[]{:S(2)}, u32[]{:S(2)}) collective-permute-start(bf16[2,2048,1024]{2,1,0:T(8,128)(2,1)} %own.13), channel_id=1, source_target_pairs={{0,1},{1,0},{2,3},{3,2},{4,5},{5,4},{6,7},{7,6},{8,9},{9,8},{10,11... | collective-permute-start | bytes 25165832 | tf_op jit(solution)/shard_map/ppermute | solution.py:70
  0.6 41.8 %collective-permute-start.7 = (bf16[1024,2048]{1,0:T(8,128)(2,1)}, bf16[1024,2048]{1,0:T(8,128)(2,1)S(1)}, u32[]{:S(2)}, u32[]{:S(2)}) collective-permute-start(bf16[1024,2048]{1,0:T(8,128)(2,1)} %own.15), channel_id=1, source_target_pairs={{0,1},{1,0},{2,3},{3,2},{4,5},{5,4},{6,7},{7,6},{8,9},{9,8},{10,11... | collective-permute-start | bytes 12582920 | tf_op jit(solution)/shard_map/ppermute | solution.py:70
  0.6 22.7 %collective-permute-start.4 = (bf16[512,2048]{1,0:T(8,128)(2,1)}, bf16[512,2048]{1,0:T(8,128)(2,1)S(1)}, u32[]{:S(2)}, u32[]{:S(2)}) collective-permute-start(bf16[512,2048]{1,0:T(8,128)(2,1)} %own.12), channel_id=1, source_target_pairs={{0,1},{1,0},{2,3},{3,2},{4,5},{5,4},{6,7},{7,6},{8,9},{9,8},{10,11... | collective-permute-start | bytes 6291464 | tf_op jit(solution)/shard_map/ppermute | solution.py:70
  6.1 5.4 %collective-permute-start = (bf16[272,128]{1,0:T(8,128)(2,1)S(1)}, bf16[272,128]{1,0:T(8,128)(2,1)S(1)}, u32[]{:S(2)}, u32[]{:S(2)}) collective-permute-start(bf16[272,128]{1,0:T(8,128)(2,1)S(1)} %get-tuple-element.27), channel_id=1, source_target_pairs={{0,4},{4,0},{8,12},{12,8},{16,20},{20,16},{24,28},{28,24},{1,5},{5... | collective-permute-start | bytes 208904 | tf_op jit(solution)/shard_map/ppermute | solution.py:80
  11.5 4.4 %collective-permute-start.1 = (bf16[272,128]{1,0:T(8,128)(2,1)S(1)}, bf16[272,128]{1,0:T(8,128)(2,1)S(1)}, u32[]{:S(2)}, u32[]{:S(2)}) collective-permute-start(bf16[272,128]{1,0:T(8,128)(2,1)S(1)} %get-tuple-element.30), channel_id=1, source_target_pairs={{0,8},{4,12},{8,0},{12,4},{16,24},{20,28},{24,16},{28,20},{1,9},{5... | collective-permute-start | bytes 208904 | tf_op jit(solution)/shard_map/ppermute | solution.py:80
  15.9 5.4 %collective-permute-start.2 = (bf16[272,128]{1,0:T(8,128)(2,1)S(1)}, bf16[272,128]{1,0:T(8,128)(2,1)S(1)}, u32[]{:S(2)}, u32[]{:S(2)}) collective-permute-start(bf16[272,128]{1,0:T(8,128)(2,1)S(1)} %get-tuple-element.33), channel_id=1, source_target_pairs={{0,16},{4,20},{8,24},{12,28},{16,0},{20,4},{24,8},{28,12},{1,17},{... | collective-permute-start | bytes 208904 | tf_op jit(solution)/shard_map/ppermute | solution.py:80
  21.4 2.0 %copy-start.2 = (bf16[512,2048]{1,0:T(8,128)(2,1)S(1)}, bf16[512,2048]{1,0:T(8,128)(2,1)}, u32[]{:S(2)}) copy-start(bf16[512,2048]{1,0:T(8,128)(2,1)} %own.12) | copy-start | bytes 6291460
  22.0 1.4 %collective-permute-start.12 = (bf16[128,512]{1,0:T(8,128)(2,1)S(1)}, bf16[128,512]{1,0:T(8,128)(2,1)S(1)}, u32[]{:S(2)}, u32[]{:S(2)}) collective-permute-start(bf16[128,512]{1,0:T(8,128)(2,1)S(1)} %finish_heads.7), channel_id=1, source_target_pairs={{0,1},{1,0},{2,3},{3,2},{4,5},{5,4},{6,7},{7,6},{8,9},{9,8},{10,11... | collective-permute-start | bytes 393224 | tf_op jit(solution)/shard_map/ppermute | solution.py:70
  23.4 16.2 %slice-start = ((s8[8388608]{0:T(1024)(128)(4,1)}), s8[4194304]{0:T(1024)(128)(4,1)S(1)}, s32[]{:S(2)}) async-start(s8[8388608]{0:T(1024)(128)(4,1)} %bitcast.3), calls=%async_computation | async-start | bytes 8388608
  24.1 15.1 %collective-permute-start.13 = (bf16[128,2048]{1,0:T(8,128)(2,1)S(1)}, bf16[128,2048]{1,0:T(8,128)(2,1)S(1)}, u32[]{:S(2)}, u32[]{:S(2)}) collective-permute-start(bf16[128,2048]{1,0:T(8,128)(2,1)S(1)} %project_heads.3.own), channel_id=1, source_target_pairs={{0,2},{1,3},{2,0},{3,1},{4,6},{5,7},{6,4},{7,5},{8,10},{9,11},{10,... | collective-permute-start | bytes 1572872 | tf_op jit(solution)/shard_map/ppermute | solution.py:75
  27.0 12.6 %slice-start.1 = ((s8[8388608]{0:T(1024)(128)(4,1)}), s8[4194304]{0:T(1024)(128)(4,1)S(1)}, s32[]{:S(2)}) async-start(s8[8388608]{0:T(1024)(128)(4,1)} %bitcast.3), calls=%async_computation.1 | async-start | bytes 8388608
  27.0 1.4 %collective-permute-start.3 = (bf16[128,512]{1,0:T(8,128)(2,1)S(1)}, bf16[128,512]{1,0:T(8,128)(2,1)S(1)}, u32[]{:S(2)}, u32[]{:S(2)}) collective-permute-start(bf16[128,512]{1,0:T(8,128)(2,1)S(1)} %finish_heads.5), channel_id=1, source_target_pairs={{0,1},{1,0},{2,3},{3,2},{4,5},{5,4},{6,7},{7,6},{8,9},{9,8},{10,11... | collective-permute-start | bytes 393224 | tf_op jit(solution)/shard_map/ppermute | solution.py:70
  27.7 11.5 %copy-start.3 = (f32[2048]{0:T(1024)S(1)}, f32[2048]{0:T(1024)}, u32[]{:S(2)}) copy-start(f32[2048]{0:T(1024)} %param.13) | copy-start | bytes 24580
  29.1 21.3 %collective-permute-start.5 = (bf16[128,2048]{1,0:T(8,128)(2,1)S(1)}, bf16[128,2048]{1,0:T(8,128)(2,1)S(1)}, u32[]{:S(2)}, u32[]{:S(2)}) collective-permute-start(bf16[128,2048]{1,0:T(8,128)(2,1)S(1)} %project_heads.2.own), channel_id=1, source_target_pairs={{0,2},{1,3},{2,0},{3,1},{4,6},{5,7},{6,4},{7,5},{8,10},{9,11},{10,... | collective-permute-start | bytes 1572872 | tf_op jit(solution)/shard_map/ppermute | solution.py:75
  39.6 2.7 %copy-start = (bf16[1024,2048]{1,0:T(8,128)(2,1)S(1)}, bf16[1024,2048]{1,0:T(8,128)(2,1)}, u32[]{:S(2)}) copy-start(bf16[1024,2048]{1,0:T(8,128)(2,1)} %own.15) | copy-start | bytes 12582916
  43.6 18.0 %collective-permute-start.14 = (bf16[128,2048]{1,0:T(8,128)(2,1)S(1)}, bf16[128,2048]{1,0:T(8,128)(2,1)S(1)}, u32[]{:S(2)}, u32[]{:S(2)}) collective-permute-start(bf16[128,2048]{1,0:T(8,128)(2,1)S(1)} %shard_map.88.own), channel_id=1, source_target_pairs={{0,2},{1,3},{2,0},{3,1},{4,6},{5,7},{6,4},{7,5},{8,10},{9,11},{10,... | collective-permute-start | bytes 1572872 | tf_op jit(solution)/shard_map/ppermute | solution.py:75
  54.0 13.2 %collective-permute-start.16 = (bf16[128,1024]{1,0:T(8,128)(2,1)S(1)}, bf16[128,1024]{1,0:T(8,128)(2,1)S(1)}, u32[]{:S(2)}, u32[]{:S(2)}) collective-permute-start(bf16[128,1024]{1,0:T(8,128)(2,1)S(1)} %shard_map.89.own), channel_id=1, source_target_pairs={{0,2},{1,3},{2,0},{3,1},{4,6},{5,7},{6,4},{7,5},{8,10},{9,11},{10,... | collective-permute-start | bytes 786440 | tf_op jit(solution)/shard_map/ppermute | solution.py:75
  61.8 12.5 %collective-permute-start.15 = (bf16[128,2048]{1,0:T(8,128)(2,1)S(1)}, bf16[128,2048]{1,0:T(8,128)(2,1)S(1)}, u32[]{:S(2)}, u32[]{:S(2)}) collective-permute-start(bf16[128,2048]{1,0:T(8,128)(2,1)S(1)} %add_partials.6.refs_0_), channel_id=1, source_target_pairs={{0,1},{1,0},{2,3},{3,2},{4,5},{5,4},{6,7},{7,6},{8,9},{9,8},{10,11... | collective-permute-start | bytes 1572872 | tf_op jit(solution)/shard_map/ppermute | solution.py:70
  62.4 7.6 %collective-permute-start.8 = (bf16[128,512]{1,0:T(8,128)(2,1)S(1)}, bf16[128,512]{1,0:T(8,128)(2,1)S(1)}, u32[]{:S(2)}, u32[]{:S(2)}) collective-permute-start(bf16[128,512]{1,0:T(8,128)(2,1)S(1)} %shard_map.85.own), channel_id=1, source_target_pairs={{0,2},{1,3},{2,0},{3,1},{4,6},{5,7},{6,4},{7,5},{8,10},{9,11},{10,... | collective-permute-start | bytes 393224 | tf_op jit(solution)/shard_map/ppermute | solution.py:75
  67.4 6.9 %collective-permute-start.17 = (bf16[128,1024]{1,0:T(8,128)(2,1)S(1)}, bf16[128,1024]{1,0:T(8,128)(2,1)S(1)}, u32[]{:S(2)}, u32[]{:S(2)}) collective-permute-start(bf16[128,1024]{1,0:T(8,128)(2,1)S(1)} %add_partials.7.refs_2_), channel_id=1, source_target_pairs={{0,1},{1,0},{2,3},{3,2},{4,5},{5,4},{6,7},{7,6},{8,9},{9,8},{10,11... | collective-permute-start | bytes 786440 | tf_op jit(solution)/shard_map/ppermute | solution.py:70
  67.9 6.2 %collective-permute-start.10 = (bf16[128,512]{1,0:T(8,128)(2,1)S(1)}, bf16[128,512]{1,0:T(8,128)(2,1)S(1)}, u32[]{:S(2)}, u32[]{:S(2)}) collective-permute-start(bf16[128,512]{1,0:T(8,128)(2,1)S(1)} %shard_map.86.own), channel_id=1, source_target_pairs={{0,2},{1,3},{2,0},{3,1},{4,6},{5,7},{6,4},{7,5},{8,10},{9,11},{10,... | collective-permute-start | bytes 393224 | tf_op jit(solution)/shard_map/ppermute | solution.py:75
  70.1 5.4 %collective-permute-start.9 = (bf16[128,512]{1,0:T(8,128)(2,1)S(1)}, bf16[128,512]{1,0:T(8,128)(2,1)S(1)}, u32[]{:S(2)}, u32[]{:S(2)}) collective-permute-start(bf16[128,512]{1,0:T(8,128)(2,1)S(1)} %add_partials.4.refs_0_), channel_id=1, source_target_pairs={{0,1},{1,0},{2,3},{3,2},{4,5},{5,4},{6,7},{7,6},{8,9},{9,8},{10,11... | collective-permute-start | bytes 393224 | tf_op jit(solution)/shard_map/ppermute | solution.py:70
  74.2 1.4 %collective-permute-start.11 = (bf16[128,512]{1,0:T(8,128)(2,1)S(1)}, bf16[128,512]{1,0:T(8,128)(2,1)S(1)}, u32[]{:S(2)}, u32[]{:S(2)}) collective-permute-start(bf16[128,512]{1,0:T(8,128)(2,1)S(1)} %add_partials.5.refs_2_), channel_id=1, source_target_pairs={{0,1},{1,0},{2,3},{3,2},{4,5},{5,4},{6,7},{7,6},{8,9},{9,8},{10,11... | collective-permute-start | bytes 393224 | tf_op jit(solution)/shard_map/ppermute | solution.py:70
  (2 other events, 3.2 us)

commit v4 on v3

--- a/solution.py
+++ b/solution.py
@@ -14,8 +14,8 @@
 log2e = 1.4426950408889634
 
 f32, bf16 = jnp.float32, jnp.bfloat16
-chunks = 2
-spans = ((1,), (2, 4, 4))
+chunks = (4, 4, 4, 4)
+spans = ((1,), (1,), (1,), (2, 2))
 
 
 vmem = pl.BlockSpec(memory_space=pltpu.VMEM)
@@ -280,11 +280,11 @@
 
 
 def heads_kernel(size, parts, side, start, q, column, before, *refs):
-    locals_, out = refs[:parts], refs[parts]
+    locals_, out = refs[:parts], refs[-1]
     span, lanes = out.shape[0], 2 * size
     width = q.shape[1] // parts
     core = own_core() if side == 0 else 1 - own_core()
-    here = pl.ds(pl.multiple_of(core * (q.shape[0] // cores) + start, span), span)
+    here = pl.ds(pl.multiple_of(core * (q.shape[0] // cores) + start, 16), span)
     ones = (iota((lanes, lanes), 0) // size == iota((lanes, lanes), 1) // size).astype(bf16)
     first = iota((size, lanes), 1) < size
     growth = jnp.exp2(spread_heads(column[here, :], size))
@@ -302,6 +302,9 @@
         low = (square - high.astype(f32)).astype(bf16)
         mean_square = (dot(high, ones) + dot(low, ones)) * (1.0 / size)
         out[:, cut] = (attended * lax.rsqrt(mean_square + head_epsilon)).astype(bf16)
+    if len(refs) > parts + 1:
+        weight, sums = refs[parts], refs[parts + 1]
+        sums[...] = dot(out[...], weight[...])
 
 
 def finish_heads(side, start, span, q, column, before, local_parts, size):
@@ -317,21 +320,34 @@
     )(q, column, before, *local_parts)
 
 
-def own_heads_kernel(kept, moved, own, partner, out):
-    out[...] = (dot(kept[...], own[...]) + dot(moved[...], partner[...])).astype(bf16)
-
-
-def project_heads(kept, moved, own, partner):
-    rows, (depth, width) = kept.shape[0], own.shape
-    return pl.pallas_call(
-        own_heads_kernel,
-        in_specs=[vmem] * 4,
-        out_specs=vmem,
-        out_shape=jax.ShapeDtypeStruct((rows, width), bf16),
-        cost_estimate=cost(4 * rows * depth * width),
+def finish_own_heads(start, span, q, column, before, local_parts, weight, size):
+    mine, width = weight.shape
+    return pl.pallas_call(
+        functools.partial(heads_kernel, size, len(local_parts), 0, start),
+        in_specs=[vmem] * (4 + len(local_parts)),
+        out_specs=vmem,
+        out_shape=jax.ShapeDtypeStruct((span, width), f32),
+        scratch_shapes=[pltpu.VMEM((span, mine), bf16)],
+        cost_estimate=cost(span * mine * 4096),
         compiler_params=room(8),
-        name="project_heads",
-    )(kept, moved, own, partner)
+        name="finish_own_heads",
+    )(q, column, before, *local_parts, weight)
+
+
+def add_heads_kernel(sums, moved, partner, out):
+    out[...] = (sums[...] + dot(moved[...], partner[...])).astype(bf16)
+
+
+def add_heads(sums, moved, partner):
+    return pl.pallas_call(
+        add_heads_kernel,
+        in_specs=[vmem] * 3,
+        out_specs=vmem,
+        out_shape=jax.ShapeDtypeStruct(sums.shape, bf16),
+        cost_estimate=cost(2 * moved.size * sums.shape[1]),
+        compiler_params=room(6),
+        name="add_heads",
+    )(sums, moved, partner)
 
 
 def residual_kernel(start, half, tok, gain, own, *refs):
@@ -340,7 +356,7 @@
     total = own[...].astype(f32)
     for other in others:
         total = total + other[...].astype(f32)
-    here = pl.ds(pl.multiple_of(own_core() * half + start, rows), rows)
+    here = pl.ds(pl.multiple_of(own_core() * half + start, 16), rows)
     total = (tok[here, :].astype(f32) + total).astype(bf16)
     residual[...] = total
     normed[...] = normalize(total.astype(f32), gain[...])
@@ -429,7 +445,7 @@
         rows, columns = pieces[2 * at].shape
         for side in range(2):
             core = own_core() if side == 0 else 1 - own_core()
-            here = pl.ds(pl.multiple_of(core * half + row, rows), rows)
+            here = pl.ds(pl.multiple_of(core * half + row, 16), rows)
             to = out.at[here, pl.ds(column, columns)]
             loads.append(pltpu.make_async_copy(pieces[2 * at + side], to, sems.at[2 * at + side]))
     for load in loads:
@@ -481,17 +497,18 @@
             others.append(value)
         return others
 
-    chunk = half // chunks
+    sizes = [half * share // 16 for share in chunks]
+    starts = [sum(sizes[:at]) for at in range(len(sizes))]
     sums = []
-    for at in range(chunks):
-        given = finish_heads(1, at * chunk, chunk, q, column, before, inside, head_size)
-        kept = finish_heads(0, at * chunk, chunk, q, column, before, inside, head_size)
+    for at, chunk in enumerate(sizes):
+        given = finish_heads(1, starts[at], chunk, q, column, before, inside, head_size)
+        kept = finish_own_heads(starts[at], chunk, q, column, before, inside, out_weight, head_size)
         moved = swap_cores(given)
-        part = project_heads(kept, moved, out_weight, out_partner)
+        part = add_heads(kept, moved, out_partner)
         sums.append((part, exchanged(part)))
     mine, theirs, spots = [], [], []
     for at, (part, others) in enumerate(sums):
-        residual, normed_ffn = add_residual(tokens, ffn_gain, part, others, at * chunk)
+        residual, normed_ffn = add_residual(tokens, ffn_gain, part, others, starts[at])
         hidden = expand(normed_ffn, expand_weight, expand_other)
         start = 0
         for parts_of in spans[at]:
@@ -500,7 +517,7 @@
             others = exchanged(partial)
             mine.append(add_partials(start, residual, partial, others))
             theirs.append(swap_cores(mine[-1]))
-            spots.append((at * chunk, start))
+            spots.append((starts[at], start))
             start += span
     late = 2
     output = place(mine[:-late], theirs[:-late], spots[:-late], tokens.shape)

time: 76.7 us -> 82.6 us (1.077)
  Pallas kernels: 23.8 us -> 38.9 us
  waiting for transfers between devices: 31 us -> 17.3 us
  starting transfers between devices: 20.7 us -> 23.5 us
  local copies, waits for them, and re-layouts: 0.55 us -> 2.14 us
    ppermute x6 -> x9, waiting for transfers between devices: 26.8 us -> 14.5 us  [across_chips(): lax.ppermute(value, 'tp', [(i, (i + cores) % count) for i in range(count)])]
    pallas_call x2 -> x4, Pallas kernels: 5.17 us -> 12.5 us  [expand(): pl.pallas_call(expand_kernel, in_specs=[vmem] * 3, out_specs=vmem, out_sh...]
    pallas_call x2 -> x8, Pallas kernels: 1.44 us -> 5.65 us  [the longest x4 3.7 us: finish_own_heads(): pl.pallas_call(functools.partial(heads_kernel, size, len(local_parts), 0,...]
    pallas_call x4 -> x5, Pallas kernels: 2.92 us -> 6.37 us  [down(): pl.pallas_call(functools.partial(down_kernel, start), in_specs=[vmem] * 3...]
    unnamed x16 -> x24, local copies, waits for them, and re-layouts: 0.55 us -> 2.14 us
    ppermute x9 -> x12, starting transfers between devices: 1.7 us -> 3.19 us  [swap_cores(): return lax.ppermute(value, 'tp', [(i, i ^ 1) for i in range(count)])]
    ppermute x9 -> x12, waiting for transfers between devices: 1.59 us -> 0.11 us  [swap_cores(): return lax.ppermute(value, 'tp', [(i, i ^ 1) for i in range(count)])]
    ppermute x6 -> x9, starting transfers between devices: 10.7 us -> 12 us  [across_chips(): lax.ppermute(value, 'tp', [(i, (i + cores) % count) for i in range(count)])]
  transfers between devices with their start and end apart: 18 -> 24, of which waited for: 11 -> 9; matrix products, arithmetic and copies ran while one was open for 0% -> 0% of each run, Pallas kernels for 30% -> 46%
where the time goes in v4:
time: 82.6 us; the launch traced here: 82.4 us
  Pallas kernels  38.9 us (47%)
  starting transfers between devices  23.5 us (28%)
  waiting for transfers between devices  17.3 us (21%)
  local copies, waits for them, and re-layouts  2.14 us (3%)
    ppermute x9, waiting for transfers between devices, across_chips(): lax.ppermute(value, 'tp', [(i, (i + cores) % count) for i in range(count)])  14.5 us
    pallas_call x4, Pallas kernels, expand(): pl.pallas_call(expand_kernel, in_specs=[vmem] * 3, out_specs=vmem, out_sh...  12.5 us
    ppermute x9, starting transfers between devices, across_chips(): lax.ppermute(value, 'tp', [(i, (i + cores) % count) for i in range(count)])  12 us
    ppermute x3, starting transfers between devices, with_seq(): return lax.ppermute(value, 'seq', [(i, i ^ bit) for i in range(count)])  8.24 us
    pallas_call x5, Pallas kernels, down(): pl.pallas_call(functools.partial(down_kernel, start), in_specs=[vmem] * 3...  6.37 us
    pallas_call x1, Pallas kernels, project(): pl.pallas_call(functools.partial(project_kernel, size), in_specs=[hbm, vm...  4.46 us
    pallas_call x4, Pallas kernels, finish_own_heads(): pl.pallas_call(functools.partial(heads_kernel, size, len(local_parts), 0,...  3.7 us
    ppermute x12, starting transfers between devices, swap_cores(): return lax.ppermute(value, 'tp', [(i, i ^ 1) for i in range(count)])  3.19 us
  transfers between devices with their start and end apart: 24, of which 9 were waited for; matrix products, arithmetic and copies ran while one was open for 0% of the time, Pallas kernels for 46%

profile of v4, /device:TPU:0, one launch (start us, length us, event | category | flops | bytes accessed | tf_op | source)
XLA Modules:
  0.0 82.4 jit_solution(18132771195389451991)
XLA Ops:
  1.6 4.5 %project.1 = (bf16[512,512]{1,0:T(8,128)(2,1)S(1)}, bf16[512,512]{1,0:T(8,128)(2,1)S(1)}, bf16[512,2048]{1,0:T(8,128)(2,1)S(1)}, bf16[2048,512]{1,0:T(8,128)(2,1...) custom-call(f32[8,128]{1,0:T(8,128)S(1)} %opening.1.opened, ...), custom_call_target="tpu_custom_call" | custom-call | flops 2147483648 | tf_op jit(solution)/shard_map/project/pallas_call | solution.py:159
  7.7 3.0 %collective-permute-start = (bf16[272,128]{1,0:T(8,128)(2,1)S(1)}, bf16[272,128]{1,0:T(8,128)(2,1)S(1)}, u32[]{:S(2)}, u32[]{:S(2)}) collective-permute-start(bf16[272,128]{1,0:T(8,128)(2,1)S(1)} %get-tuple-element.31), channel_id=1, source_target_pairs={{0,4},{4,0},{8,12},{12,8},{16,20},{20,16},{24,28},{28,24},{1,5},{5... | collective-permute-start | bytes 208904 | tf_op jit(solution)/shard_map/ppermute | solution.py:80
  10.7 1.2 %queries.1.q = bf16[512,512]{1,0:T(8,128)(2,1)S(1)} custom-call(bf16[512,2048]{1,0:T(8,128)(2,1)S(1)} %get-tuple-element.27.normed, bf16[2048,512]{1,0:T(8,128)(2,1)S(1)} %get-tuple-element.28.weight), custom_call_target="tpu_custom_call" | custom-call | flops 1073741824 | tf_op jit(solution)/shard_map/queries/pallas_call | solution.py:181
  13.0 2.1 %collective-permute-start.1 = (bf16[272,128]{1,0:T(8,128)(2,1)S(1)}, bf16[272,128]{1,0:T(8,128)(2,1)S(1)}, u32[]{:S(2)}, u32[]{:S(2)}) collective-permute-start(bf16[272,128]{1,0:T(8,128)(2,1)S(1)} %get-tuple-element.34), channel_id=1, source_target_pairs={{0,8},{4,12},{8,0},{12,4},{16,24},{20,28},{24,16},{28,20},{1,9},{5... | collective-permute-start | bytes 208904 | tf_op jit(solution)/shard_map/ppermute | solution.py:80
  15.1 1.5 %shard_map.83.refs_1_ = f32[512,256]{1,0:T(8,128)S(1)} custom-call(bf16[512,512]{1,0:T(8,128)(2,1)S(1)} %queries.1.q, bf16[512,512]{1,0:T(8,128)(2,1)S(1)} %copy-done.7, bf16[512,512]{1,0:T(8,128)(2,1)S(1)} %copy-done.9, f32[512,8]{1,0:T(8,128)S(1)} %get-tuple-element.29.column, f32[8,512]{1,0:T(8,128)S(1)} %get-tuple-element.40.row), custom_call_target="tpu_custom_call" | custom-call | flops 1073741824 | tf_op jit(solution)/shard_map/pallas_call | solution.py:224
  17.5 3.1 %collective-permute-start.2 = (bf16[272,128]{1,0:T(8,128)(2,1)S(1)}, bf16[272,128]{1,0:T(8,128)(2,1)S(1)}, u32[]{:S(2)}, u32[]{:S(2)}) collective-permute-start(bf16[272,128]{1,0:T(8,128)(2,1)S(1)} %get-tuple-element.37), channel_id=1, source_target_pairs={{0,16},{4,20},{8,24},{12,28},{16,0},{20,4},{24,8},{28,12},{1,17},{... | collective-permute-start | bytes 208904 | tf_op jit(solution)/shard_map/ppermute | solution.py:80
  20.6 1.5 %shard_map.82.refs_0_ = f32[512,256]{1,0:T(8,128)S(1)} custom-call(bf16[512,512]{1,0:T(8,128)(2,1)S(1)} %queries.1.q, bf16[512,512]{1,0:T(8,128)(2,1)S(1)} %copy-done.7, bf16[512,512]{1,0:T(8,128)(2,1)S(1)} %copy-done.9, f32[512,8]{1,0:T(8,128)S(1)} %get-tuple-element.29.column, f32[8,512]{1,0:T(8,128)S(1)} %get-tuple-element.40.row), custom_call_target="tpu_custom_call" | custom-call | flops 1073741824 | tf_op jit(solution)/shard_map/pallas_call | solution.py:224
  28.6 1.9 %collective-permute-start.21 = (bf16[64,2048]{1,0:T(8,128)(2,1)S(1)}, bf16[64,2048]{1,0:T(8,128)(2,1)S(1)}, u32[]{:S(2)}, u32[]{:S(2)}) collective-permute-start(bf16[64,2048]{1,0:T(8,128)(2,1)S(1)} %add_heads.7.own), channel_id=1, source_target_pairs={{0,2},{1,3},{2,0},{3,1},{4,6},{5,7},{6,4},{7,5},{8,10},{9,11},{10,... | collective-permute-start | bytes 786440 | tf_op jit(solution)/shard_map/ppermute | solution.py:75
  32.7 1.9 %collective-permute-start.13 = (bf16[64,2048]{1,0:T(8,128)(2,1)S(1)}, bf16[64,2048]{1,0:T(8,128)(2,1)S(1)}, u32[]{:S(2)}, u32[]{:S(2)}) collective-permute-start(bf16[64,2048]{1,0:T(8,128)(2,1)S(1)} %add_heads.5.own), channel_id=1, source_target_pairs={{0,2},{1,3},{2,0},{3,1},{4,6},{5,7},{6,4},{7,5},{8,10},{9,11},{10,... | collective-permute-start | bytes 786440 | tf_op jit(solution)/shard_map/ppermute | solution.py:75
  36.0 1.8 %collective-permute-done.21.refs_0_ = bf16[64,2048]{1,0:T(8,128)(2,1)S(1)} collective-permute-done((bf16[64,2048]{1,0:T(8,128)(2,1)S(1)}, bf16[64,2048]{1,0:T(8,128)(2,1)S(1)}, u32[]{:S(2)}, u32[]{:S(2)}) %collective-permute-start.21) | collective-permute-done | bytes 262176 | tf_op jit(solution)/shard_map/ppermute | solution.py:75
  37.9 1.8 %collective-permute-start.5 = (bf16[64,2048]{1,0:T(8,128)(2,1)S(1)}, bf16[64,2048]{1,0:T(8,128)(2,1)S(1)}, u32[]{:S(2)}, u32[]{:S(2)}) collective-permute-start(bf16[64,2048]{1,0:T(8,128)(2,1)S(1)} %add_heads.4.own), channel_id=1, source_target_pairs={{0,2},{1,3},{2,0},{3,1},{4,6},{5,7},{6,4},{7,5},{8,10},{9,11},{10,... | collective-permute-start | bytes 786440 | tf_op jit(solution)/shard_map/ppermute | solution.py:75
  40.1 3.4 %collective-permute-done.17.refs_0_ = bf16[64,2048]{1,0:T(8,128)(2,1)S(1)} collective-permute-done((bf16[64,2048]{1,0:T(8,128)(2,1)S(1)}, bf16[64,2048]{1,0:T(8,128)(2,1)S(1)}, u32[]{:S(2)}, u32[]{:S(2)}) %collective-permute-start.17) | collective-permute-done | bytes 262176 | tf_op jit(solution)/shard_map/ppermute | solution.py:75
  43.7 5.4 %collective-permute-done.13.refs_0_ = bf16[64,2048]{1,0:T(8,128)(2,1)S(1)} collective-permute-done((bf16[64,2048]{1,0:T(8,128)(2,1)S(1)}, bf16[64,2048]{1,0:T(8,128)(2,1)S(1)}, u32[]{:S(2)}, u32[]{:S(2)}) %collective-permute-start.13) | collective-permute-done | bytes 262176 | tf_op jit(solution)/shard_map/ppermute | solution.py:75
  49.4 3.1 %expand.6.hidden = bf16[64,2048]{1,0:T(8,128)(2,1)S(1)} custom-call(bf16[64,2048]{1,0:T(8,128)(2,1)S(1)} %get-tuple-element.46.rows_in, bf16[2,2048,1024]{2,1,0:T(8,128)(2,1)S(1)} %bitcast.4, bf16[2,2048,1024]{2,1,0:T(8,128)(2,1)S(1)} %collective-permute-done.6.other), custom_call_target="tpu_custom_call" | custom-call | flops 1073741824 | tf_op jit(solution)/shard_map/expand/pallas_call | solution.py:392
  52.5 1.6 %shard_map.90.own = bf16[64,2048]{1,0:T(8,128)(2,1)S(1)} custom-call(bf16[64,2048]{1,0:T(8,128)(2,1)S(1)} %expand.6.hidden, bf16[1024,2048]{1,0:T(8,128)(2,1)S(1)} %copy-done, bf16[1024,2048]{1,0:T(8,128)(2,1)S(1)} %collective-permute-done.7.other), custom_call_target="tpu_custom_call" | custom-call | flops 536870912 | tf_op jit(solution)/shard_map/pallas_call | solution.py:411
  54.1 1.9 %collective-permute-start.18 = (bf16[64,2048]{1,0:T(8,128)(2,1)S(1)}, bf16[64,2048]{1,0:T(8,128)(2,1)S(1)}, u32[]{:S(2)}, u32[]{:S(2)}) collective-permute-start(bf16[64,2048]{1,0:T(8,128)(2,1)S(1)} %shard_map.90.own), channel_id=1, source_target_pairs={{0,2},{1,3},{2,0},{3,1},{4,6},{5,7},{6,4},{7,5},{8,10},{9,11},{10,... | collective-permute-start | bytes 786440 | tf_op jit(solution)/shard_map/ppermute | solution.py:75
  56.0 3.1 %expand.5.hidden = bf16[64,2048]{1,0:T(8,128)(2,1)S(1)} custom-call(bf16[64,2048]{1,0:T(8,128)(2,1)S(1)} %get-tuple-element.44.rows_in, bf16[2,2048,1024]{2,1,0:T(8,128)(2,1)S(1)} %bitcast.4, bf16[2,2048,1024]{2,1,0:T(8,128)(2,1)S(1)} %collective-permute-done.6.other), custom_call_target="tpu_custom_call" | custom-call | flops 1073741824 | tf_op jit(solution)/shard_map/expand/pallas_call | solution.py:392
  59.0 1.6 %shard_map.88.own = bf16[64,2048]{1,0:T(8,128)(2,1)S(1)} custom-call(bf16[64,2048]{1,0:T(8,128)(2,1)S(1)} %expand.5.hidden, bf16[1024,2048]{1,0:T(8,128)(2,1)S(1)} %copy-done, bf16[1024,2048]{1,0:T(8,128)(2,1)S(1)} %collective-permute-done.7.other), custom_call_target="tpu_custom_call" | custom-call | flops 536870912 | tf_op jit(solution)/shard_map/pallas_call | solution.py:411
  60.9 3.1 %expand.7.hidden = bf16[64,2048]{1,0:T(8,128)(2,1)S(1)} custom-call(bf16[64,2048]{1,0:T(8,128)(2,1)S(1)} %get-tuple-element.48.rows_in, bf16[2,2048,1024]{2,1,0:T(8,128)(2,1)S(1)} %bitcast.4, bf16[2,2048,1024]{2,1,0:T(8,128)(2,1)S(1)} %collective-permute-done.6.other), custom_call_target="tpu_custom_call" | custom-call | flops 1073741824 | tf_op jit(solution)/shard_map/expand/pallas_call | solution.py:392
  63.9 1.6 %shard_map.92.own = bf16[64,2048]{1,0:T(8,128)(2,1)S(1)} custom-call(bf16[64,2048]{1,0:T(8,128)(2,1)S(1)} %expand.7.hidden, bf16[1024,2048]{1,0:T(8,128)(2,1)S(1)} %copy-done, bf16[1024,2048]{1,0:T(8,128)(2,1)S(1)} %collective-permute-done.7.other), custom_call_target="tpu_custom_call" | custom-call | flops 536870912 | tf_op jit(solution)/shard_map/pallas_call | solution.py:411
  65.5 1.9 %collective-permute-start.22 = (bf16[64,2048]{1,0:T(8,128)(2,1)S(1)}, bf16[64,2048]{1,0:T(8,128)(2,1)S(1)}, u32[]{:S(2)}, u32[]{:S(2)}) collective-permute-start(bf16[64,2048]{1,0:T(8,128)(2,1)S(1)} %shard_map.92.own), channel_id=1, source_target_pairs={{0,2},{1,3},{2,0},{3,1},{4,6},{5,7},{6,4},{7,5},{8,10},{9,11},{10,... | collective-permute-start | bytes 786440 | tf_op jit(solution)/shard_map/ppermute | solution.py:75
  67.7 3.3 %expand.4.hidden = bf16[64,2048]{1,0:T(8,128)(2,1)S(1)} custom-call(bf16[64,2048]{1,0:T(8,128)(2,1)S(1)} %get-tuple-element.42.rows_in, bf16[2,2048,1024]{2,1,0:T(8,128)(2,1)S(1)} %bitcast.4, bf16[2,2048,1024]{2,1,0:T(8,128)(2,1)S(1)} %collective-permute-done.6.other), custom_call_target="tpu_custom_call" | custom-call | flops 1073741824 | tf_op jit(solution)/shard_map/expand/pallas_call | solution.py:392
  74.0 1.9 %collective-permute-start.10 = (bf16[64,1024]{1,0:T(8,128)(2,1)S(1)}, bf16[64,1024]{1,0:T(8,128)(2,1)S(1)}, u32[]{:S(2)}, u32[]{:S(2)}) collective-permute-start(bf16[64,1024]{1,0:T(8,128)(2,1)S(1)} %shard_map.86.own), channel_id=1, source_target_pairs={{0,2},{1,3},{2,0},{3,1},{4,6},{5,7},{6,4},{7,5},{8,10},{9,11},{10,... | collective-permute-start | bytes 393224 | tf_op jit(solution)/shard_map/ppermute | solution.py:75
  77.0 3.0 %collective-permute-done.10.refs_0_ = bf16[64,1024]{1,0:T(8,128)(2,1)S(1)} collective-permute-done((bf16[64,1024]{1,0:T(8,128)(2,1)S(1)}, bf16[64,1024]{1,0:T(8,128)(2,1)S(1)}, u32[]{:S(2)}, u32[]{:S(2)}) %collective-permute-start.10) | collective-permute-done | bytes 131104 | tf_op jit(solution)/shard_map/ppermute | solution.py:75
  (89 shorter events, 23.0 us)
Async XLA Ops:
  0.0 49.4 %collective-permute-start.6 = (bf16[2,2048,1024]{2,1,0:T(8,128)(2,1)}, bf16[2,2048,1024]{2,1,0:T(8,128)(2,1)S(1)}, u32[]{:S(2)}, u32[]{:S(2)}) collective-permute-start(bf16[2,2048,1024]{2,1,0:T(8,128)(2,1)} %own.16), channel_id=1, source_target_pairs={{0,1},{1,0},{2,3},{3,2},{4,5},{5,4},{6,7},{7,6},{8,9},{9,8},{10,11... | collective-permute-start | bytes 25165832 | tf_op jit(solution)/shard_map/ppermute | solution.py:70
  0.6 51.9 %collective-permute-start.7 = (bf16[1024,2048]{1,0:T(8,128)(2,1)}, bf16[1024,2048]{1,0:T(8,128)(2,1)S(1)}, u32[]{:S(2)}, u32[]{:S(2)}) collective-permute-start(bf16[1024,2048]{1,0:T(8,128)(2,1)} %own.17), channel_id=1, source_target_pairs={{0,1},{1,0},{2,3},{3,2},{4,5},{5,4},{6,7},{7,6},{8,9},{9,8},{10,11... | collective-permute-start | bytes 12582920 | tf_op jit(solution)/shard_map/ppermute | solution.py:70
  0.6 25.0 %collective-permute-start.4 = (bf16[512,2048]{1,0:T(8,128)(2,1)}, bf16[512,2048]{1,0:T(8,128)(2,1)S(1)}, u32[]{:S(2)}, u32[]{:S(2)}) collective-permute-start(bf16[512,2048]{1,0:T(8,128)(2,1)} %refs_2_.7), channel_id=1, source_target_pairs={{0,1},{1,0},{2,3},{3,2},{4,5},{5,4},{6,7},{7,6},{8,9},{9,8},{10,11... | collective-permute-start | bytes 6291464 | tf_op jit(solution)/shard_map/ppermute | solution.py:70
  7.7 5.3 %collective-permute-start = (bf16[272,128]{1,0:T(8,128)(2,1)S(1)}, bf16[272,128]{1,0:T(8,128)(2,1)S(1)}, u32[]{:S(2)}, u32[]{:S(2)}) collective-permute-start(bf16[272,128]{1,0:T(8,128)(2,1)S(1)} %get-tuple-element.31), channel_id=1, source_target_pairs={{0,4},{4,0},{8,12},{12,8},{16,20},{20,16},{24,28},{28,24},{1,5},{5... | collective-permute-start | bytes 208904 | tf_op jit(solution)/shard_map/ppermute | solution.py:80
  13.0 4.4 %collective-permute-start.1 = (bf16[272,128]{1,0:T(8,128)(2,1)S(1)}, bf16[272,128]{1,0:T(8,128)(2,1)S(1)}, u32[]{:S(2)}, u32[]{:S(2)}) collective-permute-start(bf16[272,128]{1,0:T(8,128)(2,1)S(1)} %get-tuple-element.34), channel_id=1, source_target_pairs={{0,8},{4,12},{8,0},{12,4},{16,24},{20,28},{24,16},{28,20},{1,9},{5... | collective-permute-start | bytes 208904 | tf_op jit(solution)/shard_map/ppermute | solution.py:80
  17.5 5.4 %collective-permute-start.2 = (bf16[272,128]{1,0:T(8,128)(2,1)S(1)}, bf16[272,128]{1,0:T(8,128)(2,1)S(1)}, u32[]{:S(2)}, u32[]{:S(2)}) collective-permute-start(bf16[272,128]{1,0:T(8,128)(2,1)S(1)} %get-tuple-element.37), channel_id=1, source_target_pairs={{0,16},{4,20},{8,24},{12,28},{16,0},{20,4},{24,8},{28,12},{1,17},{... | collective-permute-start | bytes 208904 | tf_op jit(solution)/shard_map/ppermute | solution.py:80
  23.4 1.7 %collective-permute-start.20 = (bf16[64,512]{1,0:T(8,128)(2,1)S(1)}, bf16[64,512]{1,0:T(8,128)(2,1)S(1)}, u32[]{:S(2)}, u32[]{:S(2)}) collective-permute-start(bf16[64,512]{1,0:T(8,128)(2,1)S(1)} %finish_heads.7), channel_id=1, source_target_pairs={{0,1},{1,0},{2,3},{3,2},{4,5},{5,4},{6,7},{7,6},{8,9},{9,8},{10,11... | collective-permute-start | bytes 196616 | tf_op jit(solution)/shard_map/ppermute | solution.py:70
  24.0 4.6 %collective-permute-start.16 = (bf16[64,512]{1,0:T(8,128)(2,1)S(1)}, bf16[64,512]{1,0:T(8,128)(2,1)S(1)}, u32[]{:S(2)}, u32[]{:S(2)}) collective-permute-start(bf16[64,512]{1,0:T(8,128)(2,1)S(1)} %finish_heads.6), channel_id=1, source_target_pairs={{0,1},{1,0},{2,3},{3,2},{4,5},{5,4},{6,7},{7,6},{8,9},{9,8},{10,11... | collective-permute-start | bytes 196616 | tf_op jit(solution)/shard_map/ppermute | solution.py:70
  25.1 6.8 %collective-permute-start.12 = (bf16[64,512]{1,0:T(8,128)(2,1)S(1)}, bf16[64,512]{1,0:T(8,128)(2,1)S(1)}, u32[]{:S(2)}, u32[]{:S(2)}) collective-permute-start(bf16[64,512]{1,0:T(8,128)(2,1)S(1)} %finish_heads.5), channel_id=1, source_target_pairs={{0,1},{1,0},{2,3},{3,2},{4,5},{5,4},{6,7},{7,6},{8,9},{9,8},{10,11... | collective-permute-start | bytes 196616 | tf_op jit(solution)/shard_map/ppermute | solution.py:70
  25.7 7.0 %collective-permute-start.3 = (bf16[64,512]{1,0:T(8,128)(2,1)S(1)}, bf16[64,512]{1,0:T(8,128)(2,1)S(1)}, u32[]{:S(2)}, u32[]{:S(2)}) collective-permute-start(bf16[64,512]{1,0:T(8,128)(2,1)S(1)} %finish_heads.4), channel_id=1, source_target_pairs={{0,1},{1,0},{2,3},{3,2},{4,5},{5,4},{6,7},{7,6},{8,9},{9,8},{10,11... | collective-permute-start | bytes 196616 | tf_op jit(solution)/shard_map/ppermute | solution.py:70
  28.6 9.2 %collective-permute-start.21 = (bf16[64,2048]{1,0:T(8,128)(2,1)S(1)}, bf16[64,2048]{1,0:T(8,128)(2,1)S(1)}, u32[]{:S(2)}, u32[]{:S(2)}) collective-permute-start(bf16[64,2048]{1,0:T(8,128)(2,1)S(1)} %add_heads.7.own), channel_id=1, source_target_pairs={{0,2},{1,3},{2,0},{3,1},{4,6},{5,7},{6,4},{7,5},{8,10},{9,11},{10,... | collective-permute-start | bytes 786440 | tf_op jit(solution)/shard_map/ppermute | solution.py:75
  31.9 11.6 %collective-permute-start.17 = (bf16[64,2048]{1,0:T(8,128)(2,1)S(1)}, bf16[64,2048]{1,0:T(8,128)(2,1)S(1)}, u32[]{:S(2)}, u32[]{:S(2)}) collective-permute-start(bf16[64,2048]{1,0:T(8,128)(2,1)S(1)} %add_heads.6.own), channel_id=1, source_target_pairs={{0,2},{1,3},{2,0},{3,1},{4,6},{5,7},{6,4},{7,5},{8,10},{9,11},{10,... | collective-permute-start | bytes 786440 | tf_op jit(solution)/shard_map/ppermute | solution.py:75
  32.7 16.4 %collective-permute-start.13 = (bf16[64,2048]{1,0:T(8,128)(2,1)S(1)}, bf16[64,2048]{1,0:T(8,128)(2,1)S(1)}, u32[]{:S(2)}, u32[]{:S(2)}) collective-permute-start(bf16[64,2048]{1,0:T(8,128)(2,1)S(1)} %add_heads.5.own), channel_id=1, source_target_pairs={{0,2},{1,3},{2,0},{3,1},{4,6},{5,7},{6,4},{7,5},{8,10},{9,11},{10,... | collective-permute-start | bytes 786440 | tf_op jit(solution)/shard_map/ppermute | solution.py:75
  37.9 29.5 %collective-permute-start.5 = (bf16[64,2048]{1,0:T(8,128)(2,1)S(1)}, bf16[64,2048]{1,0:T(8,128)(2,1)S(1)}, u32[]{:S(2)}, u32[]{:S(2)}) collective-permute-start(bf16[64,2048]{1,0:T(8,128)(2,1)S(1)} %add_heads.4.own), channel_id=1, source_target_pairs={{0,2},{1,3},{2,0},{3,1},{4,6},{5,7},{6,4},{7,5},{8,10},{9,11},{10,... | collective-permute-start | bytes 786440 | tf_op jit(solution)/shard_map/ppermute | solution.py:75
  54.1 18.9 %collective-permute-start.18 = (bf16[64,2048]{1,0:T(8,128)(2,1)S(1)}, bf16[64,2048]{1,0:T(8,128)(2,1)S(1)}, u32[]{:S(2)}, u32[]{:S(2)}) collective-permute-start(bf16[64,2048]{1,0:T(8,128)(2,1)S(1)} %shard_map.90.own), channel_id=1, source_target_pairs={{0,2},{1,3},{2,0},{3,1},{4,6},{5,7},{6,4},{7,5},{8,10},{9,11},{10,... | collective-permute-start | bytes 786440 | tf_op jit(solution)/shard_map/ppermute | solution.py:75
  60.6 12.5 %collective-permute-start.14 = (bf16[64,2048]{1,0:T(8,128)(2,1)S(1)}, bf16[64,2048]{1,0:T(8,128)(2,1)S(1)}, u32[]{:S(2)}, u32[]{:S(2)}) collective-permute-start(bf16[64,2048]{1,0:T(8,128)(2,1)S(1)} %shard_map.88.own), channel_id=1, source_target_pairs={{0,2},{1,3},{2,0},{3,1},{4,6},{5,7},{6,4},{7,5},{8,10},{9,11},{10,... | collective-permute-start | bytes 786440 | tf_op jit(solution)/shard_map/ppermute | solution.py:75
  65.5 8.3 %collective-permute-start.22 = (bf16[64,2048]{1,0:T(8,128)(2,1)S(1)}, bf16[64,2048]{1,0:T(8,128)(2,1)S(1)}, u32[]{:S(2)}, u32[]{:S(2)}) collective-permute-start(bf16[64,2048]{1,0:T(8,128)(2,1)S(1)} %shard_map.92.own), channel_id=1, source_target_pairs={{0,2},{1,3},{2,0},{3,1},{4,6},{5,7},{6,4},{7,5},{8,10},{9,11},{10,... | collective-permute-start | bytes 786440 | tf_op jit(solution)/shard_map/ppermute | solution.py:75
  71.8 5.0 %collective-permute-start.8 = (bf16[64,1024]{1,0:T(8,128)(2,1)S(1)}, bf16[64,1024]{1,0:T(8,128)(2,1)S(1)}, u32[]{:S(2)}, u32[]{:S(2)}) collective-permute-start(bf16[64,1024]{1,0:T(8,128)(2,1)S(1)} %shard_map.85.own), channel_id=1, source_target_pairs={{0,2},{1,3},{2,0},{3,1},{4,6},{5,7},{6,4},{7,5},{8,10},{9,11},{10,... | collective-permute-start | bytes 393224 | tf_op jit(solution)/shard_map/ppermute | solution.py:75
  73.0 7.0 %collective-permute-start.19 = (bf16[64,2048]{1,0:T(8,128)(2,1)S(1)}, bf16[64,2048]{1,0:T(8,128)(2,1)S(1)}, u32[]{:S(2)}, u32[]{:S(2)}) collective-permute-start(bf16[64,2048]{1,0:T(8,128)(2,1)S(1)} %add_partials.8.refs_2_), channel_id=1, source_target_pairs={{0,1},{1,0},{2,3},{3,2},{4,5},{5,4},{6,7},{7,6},{8,9},{9,8},{10,11... | collective-permute-start | bytes 786440 | tf_op jit(solution)/shard_map/ppermute | solution.py:70
  73.2 6.9 %collective-permute-start.15 = (bf16[64,2048]{1,0:T(8,128)(2,1)S(1)}, bf16[64,2048]{1,0:T(8,128)(2,1)S(1)}, u32[]{:S(2)}, u32[]{:S(2)}) collective-permute-start(bf16[64,2048]{1,0:T(8,128)(2,1)S(1)} %add_partials.7.refs_0_), channel_id=1, source_target_pairs={{0,1},{1,0},{2,3},{3,2},{4,5},{5,4},{6,7},{7,6},{8,9},{9,8},{10,11... | collective-permute-start | bytes 786440 | tf_op jit(solution)/shard_map/ppermute | solution.py:70
  73.9 6.2 %collective-permute-start.23 = (bf16[64,2048]{1,0:T(8,128)(2,1)S(1)}, bf16[64,2048]{1,0:T(8,128)(2,1)S(1)}, u32[]{:S(2)}, u32[]{:S(2)}) collective-permute-start(bf16[64,2048]{1,0:T(8,128)(2,1)S(1)} %add_partials.9.refs_4_), channel_id=1, source_target_pairs={{0,1},{1,0},{2,3},{3,2},{4,5},{5,4},{6,7},{7,6},{8,9},{9,8},{10,11... | collective-permute-start | bytes 786440 | tf_op jit(solution)/shard_map/ppermute | solution.py:70
  74.0 6.0 %collective-permute-start.10 = (bf16[64,1024]{1,0:T(8,128)(2,1)S(1)}, bf16[64,1024]{1,0:T(8,128)(2,1)S(1)}, u32[]{:S(2)}, u32[]{:S(2)}) collective-permute-start(bf16[64,1024]{1,0:T(8,128)(2,1)S(1)} %shard_map.86.own), channel_id=1, source_target_pairs={{0,2},{1,3},{2,0},{3,1},{4,6},{5,7},{6,4},{7,5},{8,10},{9,11},{10,... | collective-permute-start | bytes 393224 | tf_op jit(solution)/shard_map/ppermute | solution.py:75
  76.9 4.4 %collective-permute-start.9 = (bf16[64,1024]{1,0:T(8,128)(2,1)S(1)}, bf16[64,1024]{1,0:T(8,128)(2,1)S(1)}, u32[]{:S(2)}, u32[]{:S(2)}) collective-permute-start(bf16[64,1024]{1,0:T(8,128)(2,1)S(1)} %add_partials.5.refs_0_), channel_id=1, source_target_pairs={{0,1},{1,0},{2,3},{3,2},{4,5},{5,4},{6,7},{7,6},{8,9},{9,8},{10,11... | collective-permute-start | bytes 393224 | tf_op jit(solution)/shard_map/ppermute | solution.py:70
  80.0 1.4 %collective-permute-start.11 = (bf16[64,1024]{1,0:T(8,128)(2,1)S(1)}, bf16[64,1024]{1,0:T(8,128)(2,1)S(1)}, u32[]{:S(2)}, u32[]{:S(2)}) collective-permute-start(bf16[64,1024]{1,0:T(8,128)(2,1)S(1)} %add_partials.6.refs_2_), channel_id=1, source_target_pairs={{0,1},{1,0},{2,3},{3,2},{4,5},{5,4},{6,7},{7,6},{8,9},{9,8},{10,11... | collective-permute-start | bytes 393224 | tf_op jit(solution)/shard_map/ppermute | solution.py:70
  (12 other events, 49.3 us)
